TPU v7x, 512 devices: a 8x2x16 block of a 8x8x16 slice. The times are simulated.
512 devices in a mesh: energy: 2 (over y), slab: 16 (over z), orb: 8 (over x), rhs: 2 (over core).
Axes of the slice: x: 8, y: 2, z: 16, core: 2. Of those that a mesh axis runs over, the one named last changes fastest.
The devices are a block of a 8x8x16 slice.
Arguments:
- diag_blocks: float32 [64, 192, 384], P(('energy', 'slab'), 'orb'), parts along dimension 0, may hold values from -8 to 8, as said below
- couplings: float32 [64, 192, 384], P(('energy', 'slab')), parts along dimension 0, may hold values from -8 to 8
- sources: float32 [64, 128, 384], P(('energy', 'slab'), ('orb', 'rhs')), parts along dimension 0, may hold values from -8 to 8
Outputs:
- solution: float32 [64, 128, 384], P(('energy', 'slab'), ('orb', 'rhs')), parts along dimension 0
There are 2 independent parts, one for each index of `energy`. A program takes and returns all parts, laid end to end along the dimension named above; each array names one. Nothing has to cross between parts.
Inputs may be any that keep to these rules, and one draw needn't show every extreme that they name: Every diag_blocks[n] is Hermitian, and together with couplings it makes K positive definite with smallest eigenvalue 0.01 or more.
All inputs are finite; a program needn't handle non-finite values.
Results may differ from a plain program's by a relative error of at most 0.0003.
Values sent between devices are 32-bit elements; how exact they have to be, the bound alone decides.
No kernel may reach another device: no remote copies, remote signals or barrier semaphores. Data moves between devices by JAX's collectives and lax.ppermute only.
A program may use at most 128 MiB of HBM per device.

v0:
```python
import functools
import jax
import jax.numpy as jnp
from jax import lax
from jax.experimental import pallas as pl
from jax.experimental.pallas import tpu as pltpu
from jax.sharding import PartitionSpec as P


HI = lax.Precision.HIGHEST
LANES = 128
HALF = 64
SUB = 8
LIMIT = 16 * 2**20


def mm(a, b):
    return lax.dot_general(a, b, (((1,), (0,)), ((), ())), precision=HI, preferred_element_type=jnp.float32)


def mm_t(a, b):
    return lax.dot_general(a, b, (((1,), (1,)), ((), ())), precision=HI, preferred_element_type=jnp.float32)


def lanes_of(x):
    return lax.broadcasted_iota(jnp.int32, x.shape, 1)


def times_i(x):
    parts = []
    for b in range(x.shape[1] // LANES):
        blk = x[:, b * LANES : (b + 1) * LANES]
        rolled = pltpu.roll(blk, HALF, 1)
        parts.append(jnp.where(lanes_of(blk) < HALF, -rolled, rolled))
    return jnp.concatenate(parts, axis=1)


def embed(z):
    rows = []
    turned = times_i(z)
    for a in range(z.shape[0] // HALF):
        rows.append(z[a * HALF : (a + 1) * HALF])
        rows.append(turned[a * HALF : (a + 1) * HALF])
    return jnp.concatenate(rows, axis=0)


def first_rows(e):
    return jnp.concatenate([e[a * LANES : a * LANES + HALF] for a in range(e.shape[0] // LANES)], axis=0)


def blocked(x):
    v0, v1, v2 = (x[:, LANES * b : LANES * (b + 1)] for b in range(3))
    low = lanes_of(v0) < HALF
    return jnp.concatenate(
        [jnp.where(low, v0, v1), pltpu.roll(jnp.where(low, v2, v0), HALF, 1), jnp.where(low, v1, v2)], axis=1
    )


def unblocked(x):
    u0, u1, u2 = (x[:, LANES * b : LANES * (b + 1)] for b in range(3))
    low = lanes_of(u0) < HALF
    r1 = pltpu.roll(u1, HALF, 1)
    return jnp.concatenate([jnp.where(low, u0, r1), jnp.where(low, u2, u0), jnp.where(low, r1, u2)], axis=1)


def pairs(n):
    return [(a, b) for a in range(n) for b in range(a, n)]


def packed(z):
    n = z.shape[0] // HALF
    return jnp.concatenate(
        [z[a * HALF : (a + 1) * HALF, b * LANES : (b + 1) * LANES] for a, b in pairs(n)], axis=0
    )


def adjoint(block):
    t = block.T
    return jnp.concatenate([t[:HALF], -t[HALF:]], axis=1)


def unpack_to(ref, p):
    n = ref.shape[0] // HALF
    for k, (a, b) in enumerate(pairs(n)):
        block = p[k * HALF : (k + 1) * HALF]
        ref[a * HALF : (a + 1) * HALF, b * LANES : (b + 1) * LANES] = block
        if a != b:
            ref[b * HALF : (b + 1) * HALF, a * LANES : (a + 1) * LANES] = adjoint(block)


def lane_copy(x, lane):
    return jnp.broadcast_to(x[:, lane : lane + 1], (SUB, LANES))


def row_copy(x, row):
    return jnp.broadcast_to(x[row : row + 1, :], (SUB, LANES))


def invert(buf):
    nb = buf.shape[1] // HALF
    groups = HALF // SUB
    lane = lax.broadcasted_iota(jnp.int32, (SUB, LANES), 1)
    sub = lax.broadcasted_iota(jnp.int32, (SUB, LANES), 0)
    low = lane < HALF
    lane_in = jnp.where(low, lane, lane - HALF)

    def at(a, b):
        return (slice(a * HALF, (a + 1) * HALF), slice(b * LANES, (b + 1) * LANES))

    def update(x, t, over, zs, ys):
        cols = (lane_in >= SUB * t) & (lane_in < SUB * (t + 1))
        for g in over:
            lr = [lane_copy(x[g][0], SUB * t + j) for j in range(SUB)]
            li = [lane_copy(x[g][0], HALF + SUB * t + j) for j in range(SUB)]
            new = []
            for b in range(nb):
                base = jnp.where(cols, 0.0, x[g][b]) if b == 0 else x[g][b]
                acc = [lr[j] * zs[j][b] + li[j] * ys[j][b] for j in range(SUB)]
                while len(acc) > 1:
                    acc = [acc[i] + acc[i + 1] for i in range(0, len(acc), 2)]
                new.append(base - acc[0])
            x[g] = new

    def step(i, carry):
        cur, nxt = buf.at[lax.rem(i, 2)], buf.at[lax.rem(i + 1, 2)]
        x = [
            [cur[g * SUB : (g + 1) * SUB, b * LANES : (b + 1) * LANES] for b in range(nb)] for g in range(groups)
        ]
        for t in range(groups):
            z = list(x[t])
            y = [times_i(block) for block in z]
            vr = [lane_copy(z[0], SUB * t + j) for j in range(SUB)]
            vi = [lane_copy(z[0], HALF + SUB * t + j) for j in range(SUB)]
            for p in range(SUB):
                here = sub == p
                col = lane_in == SUB * t + p
                rinv = 1.0 / row_copy(vr[p], p)
                fr = jnp.where(here, 1.0 - rinv, vr[p] * rinv)
                fi = jnp.where(here, 0.0, vi[p] * rinv)
                for j in range(p + 1, SUB):
                    ar, ai = row_copy(vr[j], p), row_copy(vi[j], p)
                    vr[j] = vr[j] - (fr * ar - fi * ai)
                    vi[j] = vi[j] - (fr * ai + fi * ar)
                unit = jnp.where(here, 1.0, 0.0)
                z[0] = jnp.where(col, jnp.where(low, unit, 0.0), z[0])
                y[0] = jnp.where(col, jnp.where(low, 0.0, unit), y[0])
                for b in range(nb):
                    zr, yr = row_copy(z[b], p), row_copy(y[b], p)
                    z[b], y[b] = z[b] - (fr * zr + fi * yr), y[b] - (fr * yr - fi * zr)
            x[t] = z
            zs = [[row_copy(z[b], j) for b in range(nb)] for j in range(SUB)]
            ys = [[row_copy(y[b], j) for b in range(nb)] for j in range(SUB)]
            update(x, t, [(t + 1 + s) % groups for s in range(groups - 1)], zs, ys)
        zp = jnp.concatenate([jnp.concatenate(x[g], axis=1) for g in range(groups)], axis=0)
        for b in range(nb):
            nxt[at(nb - 1, (b - 1) % nb)] = zp[:, b * LANES : (b + 1) * LANES]
        right = jnp.concatenate([zp, times_i(zp)], axis=0)
        change = mm(cur[HALF:, :LANES], right)
        for a in range(1, nb):
            for b in range(nb):
                piece = change[(a - 1) * HALF : a * HALF, b * LANES : (b + 1) * LANES]
                nxt[at(a - 1, (b - 1) % nb)] = -piece if b == 0 else cur[at(a, b)] - piece
        return carry

    lax.fori_loop(0, nb, step, 0)
    return buf.at[nb % 2]


def rows_times(x, z):
    blocks = [x[:, b * LANES : (b + 1) * LANES] for b in range(x.shape[1] // LANES)]
    low = lanes_of(blocks[0]) < HALF
    turned = [pltpu.roll(b, HALF, 1) for b in blocks]
    even = range(0, len(blocks) - 1, 2)
    re = [jnp.where(low, blocks[b], turned[b + 1]) for b in even]
    im = [jnp.where(low, turned[b], blocks[b + 1]) for b in even]
    if len(blocks) % 2:
        re.append(blocks[-1][:, :HALF])
        im.append(turned[-1][:, :HALF])
    both = jnp.concatenate([jnp.concatenate(re, axis=1), jnp.concatenate(im, axis=1)], axis=0)
    got = mm(both, z)
    n = x.shape[0]
    return got[:n] + times_i(got[n:])


def joined(blocks):
    return jnp.concatenate(blocks, axis=0)


def lane_blocks(z):
    return joined([z[:, b * LANES : (b + 1) * LANES] for b in range(z.shape[1] // LANES)])


def from_lane_blocks(ref, start, rows, count):
    return jnp.concatenate([ref[start + b * rows : start + (b + 1) * rows, :] for b in range(count)], axis=1)


def chained(st, rhs, steps):
    def step(i, carry):
        frm, to, which = steps(i)
        st[to] = mm(st[frm], rhs[which])
        return carry

    return step


def pivot_products(w, second, second_t, st, rhs):
    rhs[0] = embed(w)
    rhs[1] = second_t
    st[0] = second
    lax.fori_loop(0, 2, chained(st, rhs, lambda i: (i, i + 1, i)), 0)
    return st[1], st[2]


def start_kernel(diag_ref, coup_ref, w_ref, t_ref, vv_ref, buf, st, rhs):
    buf[0] = blocked(diag_ref[1])
    w = invert(buf)[...]
    w_ref[...] = w
    second = blocked(coup_ref[1])
    t, change = pivot_products(w, second, embed(second).T, st, rhs)
    t_ref[...] = t
    vv_ref[...] = packed(blocked(diag_ref[0]) - change)


def side_products(w, first_e, loads, t, st, rhs):
    order = w.shape[0]
    rhs[0] = embed(w)
    rhs[1] = first_e
    st[0, :order] = first_rows(first_e.T)
    st[0, order:] = loads
    st[2, :order] = t
    st[2, order:] = jnp.zeros_like(loads)
    lax.fori_loop(0, 3, chained(st, rhs, lambda i: (i, i + 1 + jnp.minimum(i, 1), jnp.minimum(i, 1))), 0)
    return st[1, :order], st[1, order:], st[4, :order], st[3, :order], st[3, order:]


def start_side_kernel(coup_ref, next_ref, src_ref, w_ref, t_ref, send_ref, load_ref, wl_ref, back_ref, st, rhs):
    t = t_ref[...]
    first_e = embed(blocked(next_ref[...]))
    t2, wl, uv, uu, gu = side_products(w_ref[...], first_e, blocked(src_ref[1]), t, st, rhs)
    gv = blocked(src_ref[0]) - mm_t(wl, embed(blocked(coup_ref[1])))
    load = joined([-gu, gv])
    load_ref[...] = load
    send_ref[...] = joined([lane_blocks(-uv), packed(-uu), lane_blocks(load)])
    wl_ref[...] = wl
    back_ref[...] = joined([t2, t])


def on_owner(span, body):
    def kernel(slab_ref, *refs):
        @pl.when(lax.rem(slab_ref[0], span) == 0)
        def _():
            body(*refs)

    return kernel


def merge_kernel(theirs_ref, vv_ref, send_ref, w_ref, t_ref, new_vv_ref, buf, st, rhs):
    order = w_ref.shape[0]
    count = w_ref.shape[1] // LANES
    size = vv_ref.shape[0]
    unpack_to(buf.at[0], theirs_ref[...] + send_ref[count * order : count * order + size, :])
    w = invert(buf)[...]
    w_ref[...] = w
    second = from_lane_blocks(send_ref, 0, order, count)
    t, change = pivot_products(w, second, embed(second).T, st, rhs)
    t_ref[...] = t
    new_vv_ref[...] = vv_ref[...] - packed(change)


def side_kernel(w_ref, t_ref, mine_ref, theirs_ref, send_ref, load_ref, wl_ref, back_ref, st, rhs):
    order = w_ref.shape[0]
    count = w_ref.shape[1] // LANES
    rest = count * order
    cols = load_ref.shape[0] // 2
    size = send_ref.shape[0] - rest - count * 2 * cols
    second_e = embed(from_lane_blocks(mine_ref, 0, order, count))
    my_load = from_lane_blocks(mine_ref, rest + size, 2 * cols, count)
    their_load = from_lane_blocks(theirs_ref, rest + size, 2 * cols, count)
    t = t_ref[...]
    first_e = embed(from_lane_blocks(theirs_ref, 0, order, count))
    t2, wl, uv, uu, gu = side_products(w_ref[...], first_e, their_load[cols:] + my_load[:cols], t, st, rhs)
    gv = my_load[cols:] - mm_t(wl, second_e)
    load = joined([their_load[:cols] - gu, gv])
    load_ref[...] = load
    send_ref[...] = joined([lane_blocks(-uv), theirs_ref[rest : rest + size, :] - packed(uu), lane_blocks(load)])
    wl_ref[...] = wl
    back_ref[...] = joined([t2, t])


def edge_kernel(vv_ref, send_ref, load_ref, uu_ref, h_ref, y_ref, gu_ref, buf, st, rhs):
    order, count = buf.shape[1], buf.shape[2] // LANES
    cols = y_ref.shape[0]
    size = vv_ref.shape[0]
    unpack_to(buf.at[0], vv_ref[...])
    w = invert(buf)[...]
    second_e = embed(from_lane_blocks(send_ref, 0, order, count))
    rhs[0] = embed(w)
    rhs[1] = second_e
    st[0, :order] = first_rows(second_e.T)
    st[0, order:] = load_ref[cols:, :]
    lax.fori_loop(0, 2, chained(st, rhs, lambda i: (i, i + 1, i)), 0)
    uu_ref[...] = send_ref[count * order : count * order + size, :] - packed(st[2, :order])
    h_ref[...] = st[1, :order]
    y_ref[...] = st[1, order:]
    gu_ref[...] = load_ref[:cols, :] - st[2, order:]


def last_kernel(their_vv_ref, their_load_ref, uu_ref, h_ref, y_ref, gu_ref, out_ref, vl_ref, buf):
    cols = y_ref.shape[0]
    unpack_to(buf.at[0], their_vv_ref[...] + uu_ref[...])
    w = invert(buf)[...]
    mid = rows_times(their_load_ref[cols:, :] + gu_ref[...], w)
    out_ref[...] = joined([jnp.zeros_like(mid), mid])
    vl_ref[...] = y_ref[...] - rows_times(mid, h_ref[...])


def values_of(level, slab_ref, got_ref, prev_ref, vl_ref, wl_ref, back_ref):
    cols = wl_ref.shape[0]
    span = 2 << level
    aimed = lax.rem(slab_ref[0], span) == span // 2
    vu = jnp.where(aimed, got_ref[:cols, :], prev_ref[cols:, :])
    vl = jnp.where(aimed, got_ref[cols:, :], vl_ref[...])
    mid = wl_ref[...] - rows_times(jnp.concatenate([vu, vl], axis=1), back_ref[...])
    return vu, mid, vl


def back_kernel(level, slab_ref, got_ref, prev_ref, vl_ref, wl_ref, back_ref, out_ref, new_vl_ref):
    vu, mid, vl = values_of(level, slab_ref, got_ref, prev_ref, vl_ref, wl_ref, back_ref)
    out_ref[...] = joined([vu, mid])
    new_vl_ref[...] = vl


def end_kernel(slab_ref, got_ref, prev_ref, vl_ref, wl_ref, back_ref, out_ref):
    _, mid, vl = values_of(0, slab_ref, got_ref, prev_ref, vl_ref, wl_ref, back_ref)
    out_ref[0] = unblocked(vl)
    out_ref[1] = unblocked(mid)


def f32(*shape):
    return jax.ShapeDtypeStruct(shape, jnp.float32)


def run(kernel, outs, *args, scalars=0, flops=10**8, scratch=()):
    specs = [pl.BlockSpec(memory_space=pltpu.SMEM)] * scalars
    specs += [pl.BlockSpec(memory_space=pltpu.VMEM)] * (len(args) - scalars)
    return pl.pallas_call(
        kernel,
        out_shape=outs,
        in_specs=specs,
        out_specs=jax.tree.map(lambda _: pl.BlockSpec(memory_space=pltpu.VMEM), outs),
        scratch_shapes=list(scratch),
        compiler_params=pltpu.CompilerParams(vmem_limit_bytes=LIMIT),
        cost_estimate=pl.CostEstimate(flops=flops, bytes_accessed=10**6, transcendentals=0),
    )(*args)


def forward_to(x, axis, distance):
    n = lax.axis_size(axis)
    return lax.ppermute(x, axis, [(i + distance, i) for i in range(0, n, 2 * distance)])


def back_to(x, axis, distance):
    n = lax.axis_size(axis)
    return lax.ppermute(x, axis, [(i, i + distance) for i in range(0, n, 2 * distance)])


def gathered(diag_blocks):
    layer = diag_blocks[0]
    other = diag_blocks[1]
    mine = jnp.where(lax.axis_index("rhs") == 0, layer, other)
    copies = jnp.broadcast_to(mine, (lax.axis_size("orb"), *mine.shape))
    whole = lax.all_to_all(copies, "orb", split_axis=0, concat_axis=0, tiled=True)
    return lax.all_gather(whole.reshape(-1, mine.shape[1]), "rhs")


def local(diag_blocks, couplings, sources):
    order, width = couplings.shape[1:]
    cols = sources.shape[1]
    nb = order // HALF
    size = len(pairs(nb)) * HALF
    whole = f32(order, width)
    vv_shape = f32(size, LANES)
    sides = (
        f32((order + 2 * cols) * width // LANES + size, LANES),
        f32(2 * cols, width),
        f32(cols, width),
        f32(2 * order, width),
    )
    slab = lax.axis_index("slab").astype(jnp.int32).reshape(1)
    heavy, light = 4 * 10**9, 10**9
    n = lax.axis_size("slab")
    following = lax.ppermute(couplings[0], "slab", [(i + 1, i) for i in range(n - 1)])
    levels = n.bit_length() - 1
    rhs = pltpu.VMEM((2, width, width), jnp.float32)
    buf = pltpu.VMEM((2, order, width), jnp.float32)
    for_pivot = (buf, pltpu.VMEM((3, order, width), jnp.float32), rhs)
    for_side = (pltpu.VMEM((5, order + cols, width), jnp.float32), rhs)
    for_edge = (buf, pltpu.VMEM((3, order + cols, width), jnp.float32), rhs)
    pivots = (whole, whole, vv_shape)
    pair = f32(2 * cols, width)
    one = f32(cols, width)

    def on(level, kernel, outs, *args, flops, scratch):
        return run(on_owner(1 << level, kernel), outs, slab, *args, scalars=1, flops=flops, scratch=scratch)

    w, t, vv = run(start_kernel, pivots, gathered(diag_blocks), couplings, flops=heavy, scratch=for_pivot)
    stored = []
    for level in range(levels):
        their_vv = forward_to(vv, "slab", 1 << level)
        if level == 0:
            outs = run(
                start_side_kernel, sides, couplings, following, sources, w, t, flops=light, scratch=for_side
            )
        else:
            outs = on(level, side_kernel, sides, w, t, send, theirs, flops=light, scratch=for_side)
        send, load, wl, back = outs
        stored.append((wl, back))
        if level < levels - 1:
            theirs = forward_to(send, "slab", 1 << level)
            w, t, vv = on(
                level + 1, merge_kernel, pivots, their_vv, vv, send, flops=heavy, scratch=for_pivot
            )
    theirs = forward_to(load, "slab", 1 << (levels - 1))
    edge = on(
        levels, edge_kernel, (vv_shape, whole, one, one), vv, send, load, flops=heavy, scratch=for_edge
    )
    values, vl = on(
        levels, last_kernel, (pair, one), their_vv, theirs, *edge, flops=heavy, scratch=(buf,)
    )
    for level in reversed(range(levels)):
        got = back_to(values, "slab", 1 << level)
        wl, back = stored[level]
        if level > 0:
            values, vl = run(
                functools.partial(back_kernel, level),
                (pair, one),
                slab, got, values, vl, wl, back,
                scalars=1, flops=10**7,
            )
    return run(end_kernel, f32(2, cols, width), slab, got, values, vl, wl, back, scalars=1, flops=10**7)


def solution(mesh):
    placed = (
        P(("energy", "slab"), "orb", None),
        P(("energy", "slab"), None, None),
        P(("energy", "slab"), ("orb", "rhs"), None),
    )
    return jax.shard_map(
        local,
        mesh=mesh,
        in_specs=placed,
        out_specs=P(("energy", "slab"), ("orb", "rhs"), None),
        check_vma=False,
    )
```

profile of v0, /device:TPU:66, one launch (start us, length us, event | category | flops | bytes accessed | tf_op | source)
XLA Modules:
  0.0 173.6 jit_solution(5921226983567916820)
XLA Ops:
  0.0 0.0 copy-start
  0.0 0.9 select_bitcast_fusion
  0.9 0.7 broadcast_in_dim.3
  1.6 43.7 %all-to-all-start = ((f32[8,24,384]{2,1,0:T(8,128)}), f32[8,24,384]{2,1,0:T(8,128)S(1)}, u32[]{:S(2)}, u32[]{:S(2)}) async-start(f32[8,24,384]{2,1,0:T(8,128)} %broadcast_in_dim.3), calls=%async_computation | async-start | bytes 589824 | tf_op jit(solution)/shard_map/all_to_all | solution.py:372
  45.3 0.0 copy-done
  45.4 1.3 collective-permute-start.1
  46.7 8.1 %all-to-all-done = f32[8,24,384]{2,1,0:T(8,128)S(1)} async-done(((f32[8,24,384]{2,1,0:T(8,128)}), f32[8,24,384]{2,1,0:T(8,128)S(1)}, u32[]{:S(2)}, u32[]{:S(2)}) %all-to-all-start) | async-done | bytes 294944 | tf_op jit(solution)/shard_map/all_to_all | solution.py:372
  54.8 2.2 %all_gather.3.diag_ref = f32[2,192,384]{2,1,0:T(8,128)S(1)} all-gather(f32[1,192,384]{2,1,0:T(8,128)S(1)} %bitcast.6), channel_id=1, replica_groups=mesh['energy'=2,'slab'=16,'orb'=8,'rhs'=2] {'rhs'}, dimensions={0}, use_global_device_ids=true | all-gather | bytes 884736 | tf_op jit(solution)/shard_map/all_gather | solution.py:373
  57.0 11.0 %shard_map.37 = (f32[192,384]{1,0:T(8,128)S(1)}, f32[192,384]{1,0:T(8,128)S(1)}, f32[384,128]{1,0:T(8,128)S(1)}) custom-call(f32[2,192,384]{2,1,0:T(8,128)S(1)} %all_gather.3.diag_ref, f32[2,192,384]{2,1,0:T(8,128)S(1)} %copy-done), custom_call_target="tpu_custom_call" | custom-call | flops 4000000000 | bytes 1000000 | tf_op jit(solution)/shard_map/pallas_call | solution.py:346
  68.1 1.3 collective-permute-start
  69.4 0.0 collective-permute-done.1.next_ref
  69.4 0.0 copy-done.1
  69.4 4.3 %shard_map.38 = (f32[1008,128]{1,0:T(8,128)S(1)}, f32[16,384]{1,0:T(8,128)}, f32[8,384]{1,0:T(8,128)S(1)}, f32[384,384]{1,0:T(8,128)S(1)}) custom-call(f32[2,192,384]{2,1,0:T(8,128)S(1)} %copy-done, f32[192,384]{1,0:T(8,128)S(1)} %collective-permute-done.1.next_ref, f32[2,8,384]{2,1,0:T(8,128)S(1)} %copy-done.1, f32[192,384]{1,0:T(8,128)S(1)} %get-tuple-element.43.w_ref, ...), custom_call_target="tpu_custom_call" | custom-call | flops 1000000000 | bytes 1000000 | tf_op jit(solution)/shard_map/pallas_call | solution.py:346
  73.7 1.3 collective-permute-start.3
  75.0 1.9 %collective-permute-done.refs_0_ = f32[384,128]{1,0:T(8,128)S(1)} collective-permute-done((f32[384,128]{1,0:T(8,128)S(1)}, f32[384,128]{1,0:T(8,128)S(1)}, u32[]{:S(2)}, u32[]{:S(2)}) %collective-permute-start) | collective-permute-done | bytes 196640 | tf_op jit(solution)/shard_map/ppermute | solution.py:359
  76.9 11.1 %shard_map.39 = (f32[192,384]{1,0:T(8,128)S(1)}, f32[192,384]{1,0:T(8,128)S(1)}, f32[384,128]{1,0:T(8,128)S(1)}) custom-call(s32[1]{0:T(128)} %bitcast.slab_ref, f32[384,128]{1,0:T(8,128)S(1)} %collective-permute-done.refs_0_, f32[384,128]{1,0:T(8,128)S(1)} %get-tuple-element.42.refs_1_, f32[1008,128]{1,0:T(8,128)S(1)} %get-tuple-element.45.refs_2_), custom_call_target="tpu_custom_call" | custom-call | flops 4000000000 | bytes 1000000 | tf_op jit(solution)/shard_map/pallas_call | solution.py:346
  88.0 1.3 collective-permute-start.2
  89.3 0.1 collective-permute-done.3.refs_3_
  89.4 4.2 %shard_map.40 = (f32[1008,128]{1,0:T(8,128)S(1)}, f32[16,384]{1,0:T(8,128)}, f32[8,384]{1,0:T(8,128)S(1)}, f32[384,384]{1,0:T(8,128)S(1)}) custom-call(s32[1]{0:T(128)} %bitcast.slab_ref, f32[192,384]{1,0:T(8,128)S(1)} %get-tuple-element.47.refs_0_, f32[192,384]{1,0:T(8,128)S(1)} %get-tuple-element.48.refs_1_, f32[1008,128]{1,0:T(8,128)S(1)} %get-tuple-element.45.refs_2_, ...), custom_call_target="tpu_custom_call" | custom-call | flops 1000000000 | bytes 1000000 | tf_op jit(solution)/shard_map/pallas_call | solution.py:346
  93.6 1.5 collective-permute-start.5
  95.1 1.8 %collective-permute-done.2.refs_0_ = f32[384,128]{1,0:T(8,128)S(1)} collective-permute-done((f32[384,128]{1,0:T(8,128)S(1)}, f32[384,128]{1,0:T(8,128)S(1)}, u32[]{:S(2)}, u32[]{:S(2)}) %collective-permute-start.2) | collective-permute-done | bytes 196640 | tf_op jit(solution)/shard_map/ppermute | solution.py:359
  96.9 11.1 %shard_map.41 = (f32[192,384]{1,0:T(8,128)S(1)}, f32[192,384]{1,0:T(8,128)S(1)}, f32[384,128]{1,0:T(8,128)S(1)}) custom-call(s32[1]{0:T(128)} %bitcast.slab_ref, f32[384,128]{1,0:T(8,128)S(1)} %collective-permute-done.2.refs_0_, f32[384,128]{1,0:T(8,128)S(1)} %get-tuple-element.46.refs_1_, f32[1008,128]{1,0:T(8,128)S(1)} %get-tuple-element.49.refs_2_), custom_call_target="tpu_custom_call" | custom-call | flops 4000000000 | bytes 1000000 | tf_op jit(solution)/shard_map/pallas_call | solution.py:346
  108.0 1.3 collective-permute-start.4
  109.3 0.2 collective-permute-done.5.refs_3_
  109.5 4.2 %shard_map.42 = (f32[1008,128]{1,0:T(8,128)S(1)}, f32[16,384]{1,0:T(8,128)}, f32[8,384]{1,0:T(8,128)S(1)}, f32[384,384]{1,0:T(8,128)S(1)}) custom-call(s32[1]{0:T(128)} %bitcast.slab_ref, f32[192,384]{1,0:T(8,128)S(1)} %get-tuple-element.51.refs_0_, f32[192,384]{1,0:T(8,128)S(1)} %get-tuple-element.52.refs_1_, f32[1008,128]{1,0:T(8,128)S(1)} %get-tuple-element.49.refs_2_, ...), custom_call_target="tpu_custom_call" | custom-call | flops 1000000000 | bytes 1000000 | tf_op jit(solution)/shard_map/pallas_call | solution.py:346
  113.7 1.3 collective-permute-start.7
  115.0 4.5 %collective-permute-done.4.refs_0_ = f32[384,128]{1,0:T(8,128)S(1)} collective-permute-done((f32[384,128]{1,0:T(8,128)S(1)}, f32[384,128]{1,0:T(8,128)S(1)}, u32[]{:S(2)}, u32[]{:S(2)}) %collective-permute-start.4) | collective-permute-done | bytes 196640 | tf_op jit(solution)/shard_map/ppermute | solution.py:359
  119.5 11.1 %shard_map.43 = (f32[192,384]{1,0:T(8,128)S(1)}, f32[192,384]{1,0:T(8,128)S(1)}, f32[384,128]{1,0:T(8,128)S(1)}) custom-call(s32[1]{0:T(128)} %bitcast.slab_ref, f32[384,128]{1,0:T(8,128)S(1)} %collective-permute-done.4.refs_0_, f32[384,128]{1,0:T(8,128)S(1)} %get-tuple-element.50.refs_1_, f32[1008,128]{1,0:T(8,128)S(1)} %get-tuple-element.53.refs_2_), custom_call_target="tpu_custom_call" | custom-call | flops 4000000000 | bytes 1000000 | tf_op jit(solution)/shard_map/pallas_call | solution.py:346
  130.5 1.3 collective-permute-start.6
  131.8 0.0 collective-permute-done.7.refs_3_
  131.9 3.6 %shard_map.44 = (f32[1008,128]{1,0:T(8,128)S(1)}, f32[16,384]{1,0:T(8,128)S(1)}, f32[8,384]{1,0:T(8,128)S(1)}, f32[384,384]{1,0:T(8,128)S(1)}) custom-call(s32[1]{0:T(128)} %bitcast.slab_ref, f32[192,384]{1,0:T(8,128)S(1)} %get-tuple-element.55.refs_0_, f32[192,384]{1,0:T(8,128)S(1)} %get-tuple-element.56.refs_1_, ...), custom_call_target="tpu_custom_call" | custom-call | flops 1000000000 | bytes 1000000 | tf_op jit(solution)/shard_map/pallas_call | solution.py:346
  135.5 1.3 collective-permute-start.8
  136.8 11.4 %shard_map.45 = (f32[384,128]{1,0:T(8,128)S(1)}, f32[192,384]{1,0:T(8,128)S(1)}, f32[8,384]{1,0:T(8,128)S(1)}, f32[8,384]{1,0:T(8,128)S(1)}) custom-call(s32[1]{0:T(128)} %bitcast.slab_ref, f32[384,128]{1,0:T(8,128)S(1)} %get-tuple-element.54.refs_0_, f32[1008,128]{1,0:T(8,128)S(1)} %get-tuple-element.58.refs_1_, f32[16,384]{1,0:T(8,128)S(1)} %get-tuple-element.57.refs_2_), custom_call_target="tpu_custom_call" | custom-call | flops 4000000000 | bytes 1000000 | tf_op jit(solution)/shard_map/pallas_call | solution.py:346
  148.2 0.0 collective-permute-done.6.refs_0_
  148.2 1.8 %collective-permute-done.8.refs_1_ = f32[16,384]{1,0:T(8,128)S(1)} collective-permute-done((f32[16,384]{1,0:T(8,128)S(1)}, f32[16,384]{1,0:T(8,128)S(1)}, u32[]{:S(2)}, u32[]{:S(2)}) %collective-permute-start.8) | collective-permute-done | bytes 24608 | tf_op jit(solution)/shard_map/ppermute | solution.py:359
  149.9 9.8 %shard_map.46 = (f32[16,384]{1,0:T(8,128)S(1)}, f32[8,384]{1,0:T(8,128)S(1)}) custom-call(s32[1]{0:T(128)} %bitcast.slab_ref, f32[384,128]{1,0:T(8,128)S(1)} %collective-permute-done.6.refs_0_, f32[16,384]{1,0:T(8,128)S(1)} %collective-permute-done.8.refs_1_, f32[384,128]{1,0:T(8,128)S(1)} %get-tuple-element.59.refs_2_, ...), custom_call_target="tpu_custom_call" | custom-call | flops 4000000000 | bytes 1000000 | tf_op jit(solution)/shard_map/pallas_call | solution.py:346
  159.7 1.3 collective-permute-start.9
  161.0 1.5 collective-permute-done.9.got_ref
  162.6 0.5 shard_map.47
  163.0 1.3 collective-permute-start.10
  164.3 1.5 collective-permute-done.10.got_ref
  165.8 0.5 shard_map.48
  166.3 1.3 collective-permute-start.11
  167.6 1.5 collective-permute-done.11.got_ref
  169.1 0.5 shard_map.49
  169.6 1.3 collective-permute-start.12
  170.9 1.5 collective-permute-done.12.got_ref
  172.4 1.2 shard_map.50
  (2 shorter events, 0.0 us)
Async XLA Ops:
  0.0 45.3 %copy-start = (f32[2,192,384]{2,1,0:T(8,128)S(1)}, f32[2,192,384]{2,1,0:T(8,128)}, u32[]{:S(2)}) copy-start(f32[2,192,384]{2,1,0:T(8,128)} %coup_ref.3) | copy-start | bytes 1769476
  1.6 53.2 %all-to-all-start = ((f32[8,24,384]{2,1,0:T(8,128)}), f32[8,24,384]{2,1,0:T(8,128)S(1)}, u32[]{:S(2)}, u32[]{:S(2)}) async-start(f32[8,24,384]{2,1,0:T(8,128)} %broadcast_in_dim.3), calls=%async_computation | async-start | bytes 589824 | tf_op jit(solution)/shard_map/all_to_all | solution.py:372
  45.4 24.0 %collective-permute-start.1 = (f32[192,384]{1,0:T(8,128)S(1)}, f32[192,384]{1,0:T(8,128)S(1)}, u32[]{:S(2)}, u32[]{:S(2)}) collective-permute-start(f32[192,384]{1,0:T(8,128)S(1)} %slice_bitcast_fusion), channel_id=1, source_target_pairs={{16,0},{32,16},{48,32},{64,48},{80,64},{96,80},{112,96},{128,112},... | collective-permute-start | bytes 884744 | tf_op jit(solution)/shard_map/ppermute | solution.py:392
  57.0 12.4 %copy-start.1 = (f32[2,8,384]{2,1,0:T(8,128)S(1)}, f32[2,8,384]{2,1,0:T(8,128)}, u32[]{:S(2)}) copy-start(f32[2,8,384]{2,1,0:T(8,128)} %src_ref.1) | copy-start | bytes 73732
  68.1 8.9 %collective-permute-start = (f32[384,128]{1,0:T(8,128)S(1)}, f32[384,128]{1,0:T(8,128)S(1)}, u32[]{:S(2)}, u32[]{:S(2)}) collective-permute-start(f32[384,128]{1,0:T(8,128)S(1)} %get-tuple-element.42.refs_1_), channel_id=1, source_target_pairs={{16,0},{48,32},{80,64},{112,96},{144,128},{176,160},{208,192},{240... | collective-permute-start | bytes 589832 | tf_op jit(solution)/shard_map/ppermute | solution.py:359
  73.7 15.7 %collective-permute-start.3 = (f32[1008,128]{1,0:T(8,128)S(1)}, f32[1008,128]{1,0:T(8,128)S(1)}, u32[]{:S(2)}, u32[]{:S(2)}) collective-permute-start(f32[1008,128]{1,0:T(8,128)S(1)} %get-tuple-element.45.refs_2_), channel_id=1, source_target_pairs={{16,0},{48,32},{80,64},{112,96},{144,128},{176,160},{208,192},{240... | collective-permute-start | bytes 1548296 | tf_op jit(solution)/shard_map/ppermute | solution.py:359
  88.0 8.9 %collective-permute-start.2 = (f32[384,128]{1,0:T(8,128)S(1)}, f32[384,128]{1,0:T(8,128)S(1)}, u32[]{:S(2)}, u32[]{:S(2)}) collective-permute-start(f32[384,128]{1,0:T(8,128)S(1)} %get-tuple-element.46.refs_1_), channel_id=1, source_target_pairs={{32,0},{96,64},{160,128},{224,192},{33,1},{97,65},{161,129},{225,1... | collective-permute-start | bytes 589832 | tf_op jit(solution)/shard_map/ppermute | solution.py:359
  93.6 15.8 %collective-permute-start.5 = (f32[1008,128]{1,0:T(8,128)S(1)}, f32[1008,128]{1,0:T(8,128)S(1)}, u32[]{:S(2)}, u32[]{:S(2)}) collective-permute-start(f32[1008,128]{1,0:T(8,128)S(1)} %get-tuple-element.49.refs_2_), channel_id=1, source_target_pairs={{32,0},{96,64},{160,128},{224,192},{33,1},{97,65},{161,129},{225,1... | collective-permute-start | bytes 1548296 | tf_op jit(solution)/shard_map/ppermute | solution.py:359
  108.0 11.5 %collective-permute-start.4 = (f32[384,128]{1,0:T(8,128)S(1)}, f32[384,128]{1,0:T(8,128)S(1)}, u32[]{:S(2)}, u32[]{:S(2)}) collective-permute-start(f32[384,128]{1,0:T(8,128)S(1)} %get-tuple-element.50.refs_1_), channel_id=1, source_target_pairs={{64,0},{192,128},{65,1},{193,129},{66,2},{194,130},{67,3},{195,131... | collective-permute-start | bytes 589832 | tf_op jit(solution)/shard_map/ppermute | solution.py:359
  113.7 18.2 %collective-permute-start.7 = (f32[1008,128]{1,0:T(8,128)S(1)}, f32[1008,128]{1,0:T(8,128)S(1)}, u32[]{:S(2)}, u32[]{:S(2)}) collective-permute-start(f32[1008,128]{1,0:T(8,128)S(1)} %get-tuple-element.53.refs_2_), channel_id=1, source_target_pairs={{64,0},{192,128},{65,1},{193,129},{66,2},{194,130},{67,3},{195,131... | collective-permute-start | bytes 1548296 | tf_op jit(solution)/shard_map/ppermute | solution.py:359
  130.5 17.6 %collective-permute-start.6 = (f32[384,128]{1,0:T(8,128)S(1)}, f32[384,128]{1,0:T(8,128)S(1)}, u32[]{:S(2)}, u32[]{:S(2)}) collective-permute-start(f32[384,128]{1,0:T(8,128)S(1)} %get-tuple-element.54.refs_0_), channel_id=1, source_target_pairs={{128,0},{129,1},{130,2},{131,3},{132,4},{133,5},{134,6},{135,7},{1... | collective-permute-start | bytes 589832 | tf_op jit(solution)/shard_map/ppermute | solution.py:359
  135.5 14.5 %collective-permute-start.8 = (f32[16,384]{1,0:T(8,128)S(1)}, f32[16,384]{1,0:T(8,128)S(1)}, u32[]{:S(2)}, u32[]{:S(2)}) collective-permute-start(f32[16,384]{1,0:T(8,128)S(1)} %get-tuple-element.57.refs_2_), channel_id=1, source_target_pairs={{128,0},{129,1},{130,2},{131,3},{132,4},{133,5},{134,6},{135,7},{1... | collective-permute-start | bytes 73736 | tf_op jit(solution)/shard_map/ppermute | solution.py:359
  159.7 2.8 %collective-permute-start.9 = (f32[16,384]{1,0:T(8,128)S(1)}, f32[16,384]{1,0:T(8,128)S(1)}, u32[]{:S(2)}, u32[]{:S(2)}) collective-permute-start(f32[16,384]{1,0:T(8,128)S(1)} %get-tuple-element.63.prev_ref), channel_id=1, source_target_pairs={{0,128},{1,129},{2,130},{3,131},{4,132},{5,133},{6,134},{7,135},{8... | collective-permute-start | bytes 73736 | tf_op jit(solution)/shard_map/ppermute | solution.py:364
  163.0 2.8 %collective-permute-start.10 = (f32[16,384]{1,0:T(8,128)S(1)}, f32[16,384]{1,0:T(8,128)S(1)}, u32[]{:S(2)}, u32[]{:S(2)}) collective-permute-start(f32[16,384]{1,0:T(8,128)S(1)} %get-tuple-element.67.prev_ref), channel_id=1, source_target_pairs={{0,64},{128,192},{1,65},{129,193},{2,66},{130,194},{3,67},{131,195... | collective-permute-start | bytes 73736 | tf_op jit(solution)/shard_map/ppermute | solution.py:364
  166.3 2.8 %collective-permute-start.11 = (f32[16,384]{1,0:T(8,128)S(1)}, f32[16,384]{1,0:T(8,128)S(1)}, u32[]{:S(2)}, u32[]{:S(2)}) collective-permute-start(f32[16,384]{1,0:T(8,128)S(1)} %get-tuple-element.71.prev_ref), channel_id=1, source_target_pairs={{0,32},{64,96},{128,160},{192,224},{1,33},{65,97},{129,161},{193,2... | collective-permute-start | bytes 73736 | tf_op jit(solution)/shard_map/ppermute | solution.py:364
  169.6 2.8 %collective-permute-start.12 = (f32[16,384]{1,0:T(8,128)S(1)}, f32[16,384]{1,0:T(8,128)S(1)}, u32[]{:S(2)}, u32[]{:S(2)}) collective-permute-start(f32[16,384]{1,0:T(8,128)S(1)} %get-tuple-element.75.prev_ref), channel_id=1, source_target_pairs={{0,16},{32,48},{64,80},{96,112},{128,144},{160,176},{192,208},{224... | collective-permute-start | bytes 73736 | tf_op jit(solution)/shard_map/ppermute | solution.py:364
where the time goes:
time: 174 us
  Pallas kernels  84.3 us (48%)
  starting transfers between devices  60.9 us (35%)
  waiting for transfers between devices  24.4 us (14%)
  blocking collectives  2.25 us (1%)
    pallas_call x14, Pallas kernels, run(): pl.pallas_call(kernel, out_shape=outs, in_specs=specs, out_specs=jax.tree...  84.3 us
    all_to_all x1, starting transfers between devices, gathered(): lax.all_to_all(copies, 'orb', split_axis=0, concat_axis=0, tiled=True)  43.7 us
    ppermute x8, starting transfers between devices, forward_to(): lax.ppermute(x, axis, [(i + distance, i) for i in range(0, n, 2 * distanc...  10.6 us
    ppermute x8, waiting for transfers between devices, forward_to(): lax.ppermute(x, axis, [(i + distance, i) for i in range(0, n, 2 * distanc...  10.3 us
    all_to_all x1, waiting for transfers between devices, gathered(): lax.all_to_all(copies, 'orb', split_axis=0, concat_axis=0, tiled=True)  8.11 us
    ppermute x4, waiting for transfers between devices, back_to(): lax.ppermute(x, axis, [(i, i + distance) for i in range(0, n, 2 * distanc...  6.01 us
    ppermute x4, starting transfers between devices, back_to(): lax.ppermute(x, axis, [(i, i + distance) for i in range(0, n, 2 * distanc...  5.24 us
  transfers between devices with their start and end apart: 14, of which 11 were waited for; matrix products, arithmetic and copies ran while one was open for 0% of the time, Pallas kernels for 41%

commit v1 on v0

--- a/solution.py
+++ b/solution.py
@@ -107,30 +107,14 @@
     def at(a, b):
         return (slice(a * HALF, (a + 1) * HALF), slice(b * LANES, (b + 1) * LANES))
 
-    def update(x, t, over, zs, ys):
-        cols = (lane_in >= SUB * t) & (lane_in < SUB * (t + 1))
-        for g in over:
-            lr = [lane_copy(x[g][0], SUB * t + j) for j in range(SUB)]
-            li = [lane_copy(x[g][0], HALF + SUB * t + j) for j in range(SUB)]
-            new = []
-            for b in range(nb):
-                base = jnp.where(cols, 0.0, x[g][b]) if b == 0 else x[g][b]
-                acc = [lr[j] * zs[j][b] + li[j] * ys[j][b] for j in range(SUB)]
-                while len(acc) > 1:
-                    acc = [acc[i] + acc[i + 1] for i in range(0, len(acc), 2)]
-                new.append(base - acc[0])
-            x[g] = new
-
     def step(i, carry):
         cur, nxt = buf.at[lax.rem(i, 2)], buf.at[lax.rem(i + 1, 2)]
-        x = [
-            [cur[g * SUB : (g + 1) * SUB, b * LANES : (b + 1) * LANES] for b in range(nb)] for g in range(groups)
-        ]
+        x = [cur[g * SUB : (g + 1) * SUB, :LANES] for g in range(groups)]
         for t in range(groups):
-            z = list(x[t])
-            y = [times_i(block) for block in z]
-            vr = [lane_copy(z[0], SUB * t + j) for j in range(SUB)]
-            vi = [lane_copy(z[0], HALF + SUB * t + j) for j in range(SUB)]
+            z = x[t]
+            y = times_i(z)
+            vr = [lane_copy(z, SUB * t + j) for j in range(SUB)]
+            vi = [lane_copy(z, HALF + SUB * t + j) for j in range(SUB)]
             for p in range(SUB):
                 here = sub == p
                 col = lane_in == SUB * t + p
@@ -142,20 +126,29 @@
                     vr[j] = vr[j] - (fr * ar - fi * ai)
                     vi[j] = vi[j] - (fr * ai + fi * ar)
                 unit = jnp.where(here, 1.0, 0.0)
-                z[0] = jnp.where(col, jnp.where(low, unit, 0.0), z[0])
-                y[0] = jnp.where(col, jnp.where(low, 0.0, unit), y[0])
-                for b in range(nb):
-                    zr, yr = row_copy(z[b], p), row_copy(y[b], p)
-                    z[b], y[b] = z[b] - (fr * zr + fi * yr), y[b] - (fr * yr - fi * zr)
+                z = jnp.where(col, jnp.where(low, unit, 0.0), z)
+                y = jnp.where(col, jnp.where(low, 0.0, unit), y)
+                zr, yr = row_copy(z, p), row_copy(y, p)
+                z, y = z - (fr * zr + fi * yr), y - (fr * yr - fi * zr)
             x[t] = z
-            zs = [[row_copy(z[b], j) for b in range(nb)] for j in range(SUB)]
-            ys = [[row_copy(y[b], j) for b in range(nb)] for j in range(SUB)]
-            update(x, t, [(t + 1 + s) % groups for s in range(groups - 1)], zs, ys)
-        zp = jnp.concatenate([jnp.concatenate(x[g], axis=1) for g in range(groups)], axis=0)
+            zs = [row_copy(z, j) for j in range(SUB)]
+            ys = [row_copy(y, j) for j in range(SUB)]
+            cols = (lane_in >= SUB * t) & (lane_in < SUB * (t + 1))
+            for g in [(t + 1 + s) % groups for s in range(groups - 1)]:
+                acc = [
+                    lane_copy(x[g], SUB * t + j) * zs[j] + lane_copy(x[g], HALF + SUB * t + j) * ys[j]
+                    for j in range(SUB)
+                ]
+                while len(acc) > 1:
+                    acc = [acc[q] + acc[q + 1] for q in range(0, len(acc), 2)]
+                x[g] = jnp.where(cols, 0.0, x[g]) - acc[0]
+        d = jnp.concatenate(x, axis=0)
+        rest = cur[:HALF, LANES:]
+        rest = mm(d, jnp.concatenate([rest, times_i(rest)], axis=0))
+        zp = jnp.concatenate([d, rest], axis=1)
         for b in range(nb):
             nxt[at(nb - 1, (b - 1) % nb)] = zp[:, b * LANES : (b + 1) * LANES]
-        right = jnp.concatenate([zp, times_i(zp)], axis=0)
-        change = mm(cur[HALF:, :LANES], right)
+        change = mm(cur[HALF:, :LANES], jnp.concatenate([zp, times_i(zp)], axis=0))
         for a in range(1, nb):
             for b in range(nb):
                 piece = change[(a - 1) * HALF : a * HALF, b * LANES : (b + 1) * LANES]
@@ -203,22 +196,14 @@
     return step
 
 
-def pivot_products(w, second, second_t, st, rhs):
-    rhs[0] = embed(w)
-    rhs[1] = second_t
-    st[0] = second
-    lax.fori_loop(0, 2, chained(st, rhs, lambda i: (i, i + 1, i)), 0)
-    return st[1], st[2]
-
-
-def start_kernel(diag_ref, coup_ref, w_ref, t_ref, vv_ref, buf, st, rhs):
+def start_kernel(diag_ref, coup_ref, w_ref, t_ref, vv_ref, buf):
     buf[0] = blocked(diag_ref[1])
     w = invert(buf)[...]
     w_ref[...] = w
     second = blocked(coup_ref[1])
-    t, change = pivot_products(w, second, embed(second).T, st, rhs)
+    t = mm(second, embed(w))
     t_ref[...] = t
-    vv_ref[...] = packed(blocked(diag_ref[0]) - change)
+    vv_ref[...] = packed(blocked(diag_ref[0]) - mm_t(t, embed(second)))
 
 
 def side_products(w, first_e, loads, t, st, rhs):
@@ -254,7 +239,7 @@
     return kernel
 
 
-def merge_kernel(theirs_ref, vv_ref, send_ref, w_ref, t_ref, new_vv_ref, buf, st, rhs):
+def merge_kernel(theirs_ref, vv_ref, send_ref, w_ref, t_ref, new_vv_ref, buf):
     order = w_ref.shape[0]
     count = w_ref.shape[1] // LANES
     size = vv_ref.shape[0]
@@ -262,9 +247,9 @@
     w = invert(buf)[...]
     w_ref[...] = w
     second = from_lane_blocks(send_ref, 0, order, count)
-    t, change = pivot_products(w, second, embed(second).T, st, rhs)
+    t = mm(second, embed(w))
     t_ref[...] = t
-    new_vv_ref[...] = vv_ref[...] - packed(change)
+    new_vv_ref[...] = vv_ref[...] - packed(mm_t(t, embed(second)))
 
 
 def side_kernel(w_ref, t_ref, mine_ref, theirs_ref, send_ref, load_ref, wl_ref, back_ref, st, rhs):
@@ -287,22 +272,19 @@
     back_ref[...] = joined([t2, t])
 
 
-def edge_kernel(vv_ref, send_ref, load_ref, uu_ref, h_ref, y_ref, gu_ref, buf, st, rhs):
+def edge_kernel(vv_ref, send_ref, load_ref, uu_ref, h_ref, y_ref, gu_ref, buf):
     order, count = buf.shape[1], buf.shape[2] // LANES
     cols = y_ref.shape[0]
     size = vv_ref.shape[0]
     unpack_to(buf.at[0], vv_ref[...])
     w = invert(buf)[...]
     second_e = embed(from_lane_blocks(send_ref, 0, order, count))
-    rhs[0] = embed(w)
-    rhs[1] = second_e
-    st[0, :order] = first_rows(second_e.T)
-    st[0, order:] = load_ref[cols:, :]
-    lax.fori_loop(0, 2, chained(st, rhs, lambda i: (i, i + 1, i)), 0)
-    uu_ref[...] = send_ref[count * order : count * order + size, :] - packed(st[2, :order])
-    h_ref[...] = st[1, :order]
-    y_ref[...] = st[1, order:]
-    gu_ref[...] = load_ref[:cols, :] - st[2, order:]
+    own = mm(joined([first_rows(second_e.T), load_ref[cols:, :]]), embed(w))
+    change = mm(own, second_e)
+    uu_ref[...] = send_ref[count * order : count * order + size, :] - packed(change[:order])
+    h_ref[...] = own[:order]
+    y_ref[...] = own[order:]
+    gu_ref[...] = load_ref[:cols, :] - change[order:]
 
 
 def last_kernel(their_vv_ref, their_load_ref, uu_ref, h_ref, y_ref, gu_ref, out_ref, vl_ref, buf):
@@ -365,12 +347,11 @@
 
 
 def gathered(diag_blocks):
-    layer = diag_blocks[0]
-    other = diag_blocks[1]
-    mine = jnp.where(lax.axis_index("rhs") == 0, layer, other)
-    copies = jnp.broadcast_to(mine, (lax.axis_size("orb"), *mine.shape))
+    width = diag_blocks.shape[2]
+    copies = [jnp.broadcast_to(layer, (lax.axis_size("orb"), *layer.shape)) for layer in diag_blocks]
+    copies = jnp.where(lax.axis_index("rhs") == 0, copies[0], copies[1])
     whole = lax.all_to_all(copies, "orb", split_axis=0, concat_axis=0, tiled=True)
-    return lax.all_gather(whole.reshape(-1, mine.shape[1]), "rhs")
+    return lax.all_gather(whole.reshape(-1, width), "rhs")
 
 
 def local(diag_blocks, couplings, sources):
@@ -393,9 +374,8 @@
     levels = n.bit_length() - 1
     rhs = pltpu.VMEM((2, width, width), jnp.float32)
     buf = pltpu.VMEM((2, order, width), jnp.float32)
-    for_pivot = (buf, pltpu.VMEM((3, order, width), jnp.float32), rhs)
+    for_pivot = (buf,)
     for_side = (pltpu.VMEM((5, order + cols, width), jnp.float32), rhs)
-    for_edge = (buf, pltpu.VMEM((3, order + cols, width), jnp.float32), rhs)
     pivots = (whole, whole, vv_shape)
     pair = f32(2 * cols, width)
     one = f32(cols, width)
@@ -422,10 +402,10 @@
             )
     theirs = forward_to(load, "slab", 1 << (levels - 1))
     edge = on(
-        levels, edge_kernel, (vv_shape, whole, one, one), vv, send, load, flops=heavy, scratch=for_edge
+        levels, edge_kernel, (vv_shape, whole, one, one), vv, send, load, flops=heavy, scratch=for_pivot
     )
     values, vl = on(
-        levels, last_kernel, (pair, one), their_vv, theirs, *edge, flops=heavy, scratch=(buf,)
+        levels, last_kernel, (pair, one), their_vv, theirs, *edge, flops=heavy, scratch=for_pivot
     )
     for level in reversed(range(levels)):
         got = back_to(values, "slab", 1 << level)

time: 174 us -> 173 us (level)
  Pallas kernels: 84.3 us -> 81.8 us
    pallas_call x14, Pallas kernels: 84.3 us -> 81.8 us  [run(): pl.pallas_call(kernel, out_shape=outs, in_specs=specs, out_specs=jax.tree...]
  transfers between devices with their start and end apart: 14 -> 14, of which waited for: 11 -> 12; matrix products, arithmetic and copies ran while one was open for 0% -> 0% of each run, Pallas kernels for 41% -> 40%
where the time goes in v1:
time: 173 us
  Pallas kernels  81.8 us (47%)
  starting transfers between devices  60.7 us (35%)
  waiting for transfers between devices  26.1 us (15%)
  blocking collectives  2.25 us (1%)
    pallas_call x14, Pallas kernels, run(): pl.pallas_call(kernel, out_shape=outs, in_specs=specs, out_specs=jax.tree...  81.8 us
    all_to_all x1, starting transfers between devices, gathered(): lax.all_to_all(copies, 'orb', split_axis=0, concat_axis=0, tiled=True)  43.7 us
    ppermute x8, waiting for transfers between devices, forward_to(): lax.ppermute(x, axis, [(i + distance, i) for i in range(0, n, 2 * distanc...  12 us
    ppermute x8, starting transfers between devices, forward_to(): lax.ppermute(x, axis, [(i + distance, i) for i in range(0, n, 2 * distanc...  10.4 us
    all_to_all x1, waiting for transfers between devices, gathered(): lax.all_to_all(copies, 'orb', split_axis=0, concat_axis=0, tiled=True)  8.11 us
    ppermute x4, waiting for transfers between devices, back_to(): lax.ppermute(x, axis, [(i, i + distance) for i in range(0, n, 2 * distanc...  6.01 us
    ppermute x4, starting transfers between devices, back_to(): lax.ppermute(x, axis, [(i, i + distance) for i in range(0, n, 2 * distanc...  5.24 us
  transfers between devices with their start and end apart: 14, of which 12 were waited for; matrix products, arithmetic and copies ran while one was open for 0% of the time, Pallas kernels for 40%

profile of v1, /device:TPU:66, one launch (start us, length us, event | category | flops | bytes accessed | tf_op | source)
XLA Modules:
  0.0 172.6 jit_solution(6352652866878285711)
XLA Ops:
  0.0 0.0 copy-start
  0.0 0.9 select_bitcast_fusion
  0.9 0.7 broadcast_in_dim.4
  1.6 43.7 %all-to-all-start = ((f32[8,24,384]{2,1,0:T(8,128)}), f32[8,24,384]{2,1,0:T(8,128)S(1)}, u32[]{:S(2)}, u32[]{:S(2)}) async-start(f32[8,24,384]{2,1,0:T(8,128)} %broadcast_in_dim.4), calls=%async_computation | async-start | bytes 589824 | tf_op jit(solution)/shard_map/all_to_all | solution.py:353
  45.3 0.0 copy-done
  45.4 1.3 collective-permute-start.1
  46.7 8.1 %all-to-all-done = f32[8,24,384]{2,1,0:T(8,128)S(1)} async-done(((f32[8,24,384]{2,1,0:T(8,128)}), f32[8,24,384]{2,1,0:T(8,128)S(1)}, u32[]{:S(2)}, u32[]{:S(2)}) %all-to-all-start) | async-done | bytes 294944 | tf_op jit(solution)/shard_map/all_to_all | solution.py:353
  54.8 2.2 %all_gather.3.diag_ref = f32[2,192,384]{2,1,0:T(8,128)S(1)} all-gather(f32[1,192,384]{2,1,0:T(8,128)S(1)} %bitcast.6), channel_id=1, replica_groups=mesh['energy'=2,'slab'=16,'orb'=8,'rhs'=2] {'rhs'}, dimensions={0}, use_global_device_ids=true | all-gather | bytes 884736 | tf_op jit(solution)/shard_map/all_gather | solution.py:354
  57.0 10.5 %shard_map.37 = (f32[192,384]{1,0:T(8,128)S(1)}, f32[192,384]{1,0:T(8,128)S(1)}, f32[384,128]{1,0:T(8,128)S(1)}) custom-call(f32[2,192,384]{2,1,0:T(8,128)S(1)} %all_gather.3.diag_ref, f32[2,192,384]{2,1,0:T(8,128)S(1)} %copy-done), custom_call_target="tpu_custom_call" | custom-call | flops 4000000000 | bytes 1000000 | tf_op jit(solution)/shard_map/pallas_call | solution.py:328
  67.6 1.3 collective-permute-start
  68.9 0.0 collective-permute-done.1.next_ref
  68.9 0.0 copy-done.1
  68.9 4.3 %shard_map.38 = (f32[1008,128]{1,0:T(8,128)S(1)}, f32[16,384]{1,0:T(8,128)}, f32[8,384]{1,0:T(8,128)S(1)}, f32[384,384]{1,0:T(8,128)S(1)}) custom-call(f32[2,192,384]{2,1,0:T(8,128)S(1)} %copy-done, f32[192,384]{1,0:T(8,128)S(1)} %collective-permute-done.1.next_ref, f32[2,8,384]{2,1,0:T(8,128)S(1)} %copy-done.1, f32[192,384]{1,0:T(8,128)S(1)} %get-tuple-element.43.w_ref, ...), custom_call_target="tpu_custom_call" | custom-call | flops 1000000000 | bytes 1000000 | tf_op jit(solution)/shard_map/pallas_call | solution.py:328
  73.2 1.3 collective-permute-start.3
  74.5 1.9 %collective-permute-done.refs_0_ = f32[384,128]{1,0:T(8,128)S(1)} collective-permute-done((f32[384,128]{1,0:T(8,128)S(1)}, f32[384,128]{1,0:T(8,128)S(1)}, u32[]{:S(2)}, u32[]{:S(2)}) %collective-permute-start) | collective-permute-done | bytes 196640 | tf_op jit(solution)/shard_map/ppermute | solution.py:341
  76.4 10.6 %shard_map.39 = (f32[192,384]{1,0:T(8,128)S(1)}, f32[192,384]{1,0:T(8,128)S(1)}, f32[384,128]{1,0:T(8,128)S(1)}) custom-call(s32[1]{0:T(128)} %bitcast.slab_ref, f32[384,128]{1,0:T(8,128)S(1)} %collective-permute-done.refs_0_, f32[384,128]{1,0:T(8,128)S(1)} %get-tuple-element.42.refs_1_, f32[1008,128]{1,0:T(8,128)S(1)} %get-tuple-element.45.refs_2_), custom_call_target="tpu_custom_call" | custom-call | flops 4000000000 | bytes 1000000 | tf_op jit(solution)/shard_map/pallas_call | solution.py:328
  87.0 1.3 collective-permute-start.2
  88.4 0.5 collective-permute-done.3.refs_3_
  88.9 4.2 %shard_map.40 = (f32[1008,128]{1,0:T(8,128)S(1)}, f32[16,384]{1,0:T(8,128)}, f32[8,384]{1,0:T(8,128)S(1)}, f32[384,384]{1,0:T(8,128)S(1)}) custom-call(s32[1]{0:T(128)} %bitcast.slab_ref, f32[192,384]{1,0:T(8,128)S(1)} %get-tuple-element.47.refs_0_, f32[192,384]{1,0:T(8,128)S(1)} %get-tuple-element.48.refs_1_, f32[1008,128]{1,0:T(8,128)S(1)} %get-tuple-element.45.refs_2_, ...), custom_call_target="tpu_custom_call" | custom-call | flops 1000000000 | bytes 1000000 | tf_op jit(solution)/shard_map/pallas_call | solution.py:328
  93.1 1.3 collective-permute-start.5
  94.4 1.6 collective-permute-done.2.refs_0_
  96.0 10.6 %shard_map.41 = (f32[192,384]{1,0:T(8,128)S(1)}, f32[192,384]{1,0:T(8,128)S(1)}, f32[384,128]{1,0:T(8,128)S(1)}) custom-call(s32[1]{0:T(128)} %bitcast.slab_ref, f32[384,128]{1,0:T(8,128)S(1)} %collective-permute-done.2.refs_0_, f32[384,128]{1,0:T(8,128)S(1)} %get-tuple-element.46.refs_1_, f32[1008,128]{1,0:T(8,128)S(1)} %get-tuple-element.49.refs_2_), custom_call_target="tpu_custom_call" | custom-call | flops 4000000000 | bytes 1000000 | tf_op jit(solution)/shard_map/pallas_call | solution.py:328
  106.6 1.3 collective-permute-start.4
  107.9 0.9 collective-permute-done.5.refs_3_
  108.8 4.2 %shard_map.42 = (f32[1008,128]{1,0:T(8,128)S(1)}, f32[16,384]{1,0:T(8,128)}, f32[8,384]{1,0:T(8,128)S(1)}, f32[384,384]{1,0:T(8,128)S(1)}) custom-call(s32[1]{0:T(128)} %bitcast.slab_ref, f32[192,384]{1,0:T(8,128)S(1)} %get-tuple-element.51.refs_0_, f32[192,384]{1,0:T(8,128)S(1)} %get-tuple-element.52.refs_1_, f32[1008,128]{1,0:T(8,128)S(1)} %get-tuple-element.49.refs_2_, ...), custom_call_target="tpu_custom_call" | custom-call | flops 1000000000 | bytes 1000000 | tf_op jit(solution)/shard_map/pallas_call | solution.py:328
  113.0 1.3 collective-permute-start.7
  114.3 3.8 %collective-permute-done.4.refs_0_ = f32[384,128]{1,0:T(8,128)S(1)} collective-permute-done((f32[384,128]{1,0:T(8,128)S(1)}, f32[384,128]{1,0:T(8,128)S(1)}, u32[]{:S(2)}, u32[]{:S(2)}) %collective-permute-start.4) | collective-permute-done | bytes 196640 | tf_op jit(solution)/shard_map/ppermute | solution.py:341
  118.1 10.6 %shard_map.43 = (f32[192,384]{1,0:T(8,128)S(1)}, f32[192,384]{1,0:T(8,128)S(1)}, f32[384,128]{1,0:T(8,128)S(1)}) custom-call(s32[1]{0:T(128)} %bitcast.slab_ref, f32[384,128]{1,0:T(8,128)S(1)} %collective-permute-done.4.refs_0_, f32[384,128]{1,0:T(8,128)S(1)} %get-tuple-element.50.refs_1_, f32[1008,128]{1,0:T(8,128)S(1)} %get-tuple-element.53.refs_2_), custom_call_target="tpu_custom_call" | custom-call | flops 4000000000 | bytes 1000000 | tf_op jit(solution)/shard_map/pallas_call | solution.py:328
  128.7 1.3 collective-permute-start.6
  130.0 0.9 collective-permute-done.7.refs_3_
  130.9 3.6 %shard_map.44 = (f32[1008,128]{1,0:T(8,128)S(1)}, f32[16,384]{1,0:T(8,128)S(1)}, f32[8,384]{1,0:T(8,128)S(1)}, f32[384,384]{1,0:T(8,128)S(1)}) custom-call(s32[1]{0:T(128)} %bitcast.slab_ref, f32[192,384]{1,0:T(8,128)S(1)} %get-tuple-element.55.refs_0_, f32[192,384]{1,0:T(8,128)S(1)} %get-tuple-element.56.refs_1_, ...), custom_call_target="tpu_custom_call" | custom-call | flops 1000000000 | bytes 1000000 | tf_op jit(solution)/shard_map/pallas_call | solution.py:328
  134.5 1.3 collective-permute-start.8
  135.8 10.7 %shard_map.45 = (f32[384,128]{1,0:T(8,128)S(1)}, f32[192,384]{1,0:T(8,128)S(1)}, f32[8,384]{1,0:T(8,128)S(1)}, f32[8,384]{1,0:T(8,128)S(1)}) custom-call(s32[1]{0:T(128)} %bitcast.slab_ref, f32[384,128]{1,0:T(8,128)S(1)} %get-tuple-element.54.refs_0_, f32[1008,128]{1,0:T(8,128)S(1)} %get-tuple-element.58.refs_1_, f32[16,384]{1,0:T(8,128)S(1)} %get-tuple-element.57.refs_2_), custom_call_target="tpu_custom_call" | custom-call | flops 4000000000 | bytes 1000000 | tf_op jit(solution)/shard_map/pallas_call | solution.py:328
  146.6 0.0 collective-permute-done.6.refs_0_
  146.6 2.4 %collective-permute-done.8.refs_1_ = f32[16,384]{1,0:T(8,128)S(1)} collective-permute-done((f32[16,384]{1,0:T(8,128)S(1)}, f32[16,384]{1,0:T(8,128)S(1)}, u32[]{:S(2)}, u32[]{:S(2)}) %collective-permute-start.8) | collective-permute-done | bytes 24608 | tf_op jit(solution)/shard_map/ppermute | solution.py:341
  149.0 9.8 %shard_map.46 = (f32[16,384]{1,0:T(8,128)S(1)}, f32[8,384]{1,0:T(8,128)S(1)}) custom-call(s32[1]{0:T(128)} %bitcast.slab_ref, f32[384,128]{1,0:T(8,128)S(1)} %collective-permute-done.6.refs_0_, f32[16,384]{1,0:T(8,128)S(1)} %collective-permute-done.8.refs_1_, f32[384,128]{1,0:T(8,128)S(1)} %get-tuple-element.59.refs_2_, ...), custom_call_target="tpu_custom_call" | custom-call | flops 4000000000 | bytes 1000000 | tf_op jit(solution)/shard_map/pallas_call | solution.py:328
  158.7 1.3 collective-permute-start.9
  160.1 1.5 collective-permute-done.9.got_ref
  161.6 0.5 shard_map.47
  162.0 1.3 collective-permute-start.10
  163.4 1.5 collective-permute-done.10.got_ref
  164.9 0.5 shard_map.48
  165.3 1.3 collective-permute-start.11
  166.6 1.5 collective-permute-done.11.got_ref
  168.2 0.5 shard_map.49
  168.6 1.3 collective-permute-start.12
  169.9 1.5 collective-permute-done.12.got_ref
  171.4 1.2 shard_map.50
  (2 shorter events, 0.0 us)
Async XLA Ops:
  0.0 45.3 %copy-start = (f32[2,192,384]{2,1,0:T(8,128)S(1)}, f32[2,192,384]{2,1,0:T(8,128)}, u32[]{:S(2)}) copy-start(f32[2,192,384]{2,1,0:T(8,128)} %coup_ref.3) | copy-start | bytes 1769476
  1.6 53.2 %all-to-all-start = ((f32[8,24,384]{2,1,0:T(8,128)}), f32[8,24,384]{2,1,0:T(8,128)S(1)}, u32[]{:S(2)}, u32[]{:S(2)}) async-start(f32[8,24,384]{2,1,0:T(8,128)} %broadcast_in_dim.4), calls=%async_computation | async-start | bytes 589824 | tf_op jit(solution)/shard_map/all_to_all | solution.py:353
  45.4 23.5 %collective-permute-start.1 = (f32[192,384]{1,0:T(8,128)S(1)}, f32[192,384]{1,0:T(8,128)S(1)}, u32[]{:S(2)}, u32[]{:S(2)}) collective-permute-start(f32[192,384]{1,0:T(8,128)S(1)} %slice_bitcast_fusion), channel_id=1, source_target_pairs={{16,0},{32,16},{48,32},{64,48},{80,64},{96,80},{112,96},{128,112},... | collective-permute-start | bytes 884744 | tf_op jit(solution)/shard_map/ppermute | solution.py:373
  57.0 11.9 %copy-start.1 = (f32[2,8,384]{2,1,0:T(8,128)S(1)}, f32[2,8,384]{2,1,0:T(8,128)}, u32[]{:S(2)}) copy-start(f32[2,8,384]{2,1,0:T(8,128)} %src_ref.1) | copy-start | bytes 73732
  67.6 8.9 %collective-permute-start = (f32[384,128]{1,0:T(8,128)S(1)}, f32[384,128]{1,0:T(8,128)S(1)}, u32[]{:S(2)}, u32[]{:S(2)}) collective-permute-start(f32[384,128]{1,0:T(8,128)S(1)} %get-tuple-element.42.refs_1_), channel_id=1, source_target_pairs={{16,0},{48,32},{80,64},{112,96},{144,128},{176,160},{208,192},{240... | collective-permute-start | bytes 589832 | tf_op jit(solution)/shard_map/ppermute | solution.py:341
  73.2 15.7 %collective-permute-start.3 = (f32[1008,128]{1,0:T(8,128)S(1)}, f32[1008,128]{1,0:T(8,128)S(1)}, u32[]{:S(2)}, u32[]{:S(2)}) collective-permute-start(f32[1008,128]{1,0:T(8,128)S(1)} %get-tuple-element.45.refs_2_), channel_id=1, source_target_pairs={{16,0},{48,32},{80,64},{112,96},{144,128},{176,160},{208,192},{240... | collective-permute-start | bytes 1548296 | tf_op jit(solution)/shard_map/ppermute | solution.py:341
  87.0 8.9 %collective-permute-start.2 = (f32[384,128]{1,0:T(8,128)S(1)}, f32[384,128]{1,0:T(8,128)S(1)}, u32[]{:S(2)}, u32[]{:S(2)}) collective-permute-start(f32[384,128]{1,0:T(8,128)S(1)} %get-tuple-element.46.refs_1_), channel_id=1, source_target_pairs={{32,0},{96,64},{160,128},{224,192},{33,1},{97,65},{161,129},{225,1... | collective-permute-start | bytes 589832 | tf_op jit(solution)/shard_map/ppermute | solution.py:341
  93.1 15.7 %collective-permute-start.5 = (f32[1008,128]{1,0:T(8,128)S(1)}, f32[1008,128]{1,0:T(8,128)S(1)}, u32[]{:S(2)}, u32[]{:S(2)}) collective-permute-start(f32[1008,128]{1,0:T(8,128)S(1)} %get-tuple-element.49.refs_2_), channel_id=1, source_target_pairs={{32,0},{96,64},{160,128},{224,192},{33,1},{97,65},{161,129},{225,1... | collective-permute-start | bytes 1548296 | tf_op jit(solution)/shard_map/ppermute | solution.py:341
  106.6 11.5 %collective-permute-start.4 = (f32[384,128]{1,0:T(8,128)S(1)}, f32[384,128]{1,0:T(8,128)S(1)}, u32[]{:S(2)}, u32[]{:S(2)}) collective-permute-start(f32[384,128]{1,0:T(8,128)S(1)} %get-tuple-element.50.refs_1_), channel_id=1, source_target_pairs={{64,0},{192,128},{65,1},{193,129},{66,2},{194,130},{67,3},{195,131... | collective-permute-start | bytes 589832 | tf_op jit(solution)/shard_map/ppermute | solution.py:341
  113.0 17.9 %collective-permute-start.7 = (f32[1008,128]{1,0:T(8,128)S(1)}, f32[1008,128]{1,0:T(8,128)S(1)}, u32[]{:S(2)}, u32[]{:S(2)}) collective-permute-start(f32[1008,128]{1,0:T(8,128)S(1)} %get-tuple-element.53.refs_2_), channel_id=1, source_target_pairs={{64,0},{192,128},{65,1},{193,129},{66,2},{194,130},{67,3},{195,131... | collective-permute-start | bytes 1548296 | tf_op jit(solution)/shard_map/ppermute | solution.py:341
  128.7 17.8 %collective-permute-start.6 = (f32[384,128]{1,0:T(8,128)S(1)}, f32[384,128]{1,0:T(8,128)S(1)}, u32[]{:S(2)}, u32[]{:S(2)}) collective-permute-start(f32[384,128]{1,0:T(8,128)S(1)} %get-tuple-element.54.refs_0_), channel_id=1, source_target_pairs={{128,0},{129,1},{130,2},{131,3},{132,4},{133,5},{134,6},{135,7},{1... | collective-permute-start | bytes 589832 | tf_op jit(solution)/shard_map/ppermute | solution.py:341
  134.5 14.5 %collective-permute-start.8 = (f32[16,384]{1,0:T(8,128)S(1)}, f32[16,384]{1,0:T(8,128)S(1)}, u32[]{:S(2)}, u32[]{:S(2)}) collective-permute-start(f32[16,384]{1,0:T(8,128)S(1)} %get-tuple-element.57.refs_2_), channel_id=1, source_target_pairs={{128,0},{129,1},{130,2},{131,3},{132,4},{133,5},{134,6},{135,7},{1... | collective-permute-start | bytes 73736 | tf_op jit(solution)/shard_map/ppermute | solution.py:341
  158.7 2.8 %collective-permute-start.9 = (f32[16,384]{1,0:T(8,128)S(1)}, f32[16,384]{1,0:T(8,128)S(1)}, u32[]{:S(2)}, u32[]{:S(2)}) collective-permute-start(f32[16,384]{1,0:T(8,128)S(1)} %get-tuple-element.63.prev_ref), channel_id=1, source_target_pairs={{0,128},{1,129},{2,130},{3,131},{4,132},{5,133},{6,134},{7,135},{8... | collective-permute-start | bytes 73736 | tf_op jit(solution)/shard_map/ppermute | solution.py:346
  162.0 2.8 %collective-permute-start.10 = (f32[16,384]{1,0:T(8,128)S(1)}, f32[16,384]{1,0:T(8,128)S(1)}, u32[]{:S(2)}, u32[]{:S(2)}) collective-permute-start(f32[16,384]{1,0:T(8,128)S(1)} %get-tuple-element.67.prev_ref), channel_id=1, source_target_pairs={{0,64},{128,192},{1,65},{129,193},{2,66},{130,194},{3,67},{131,195... | collective-permute-start | bytes 73736 | tf_op jit(solution)/shard_map/ppermute | solution.py:346
  165.3 2.8 %collective-permute-start.11 = (f32[16,384]{1,0:T(8,128)S(1)}, f32[16,384]{1,0:T(8,128)S(1)}, u32[]{:S(2)}, u32[]{:S(2)}) collective-permute-start(f32[16,384]{1,0:T(8,128)S(1)} %get-tuple-element.71.prev_ref), channel_id=1, source_target_pairs={{0,32},{64,96},{128,160},{192,224},{1,33},{65,97},{129,161},{193,2... | collective-permute-start | bytes 73736 | tf_op jit(solution)/shard_map/ppermute | solution.py:346
  168.6 2.8 %collective-permute-start.12 = (f32[16,384]{1,0:T(8,128)S(1)}, f32[16,384]{1,0:T(8,128)S(1)}, u32[]{:S(2)}, u32[]{:S(2)}) collective-permute-start(f32[16,384]{1,0:T(8,128)S(1)} %get-tuple-element.75.prev_ref), channel_id=1, source_target_pairs={{0,16},{32,48},{64,80},{96,112},{128,144},{160,176},{192,208},{224... | collective-permute-start | bytes 73736 | tf_op jit(solution)/shard_map/ppermute | solution.py:346

commit v2 on v1

--- a/solution.py
+++ b/solution.py
@@ -64,14 +64,55 @@
 
 
 def pairs(n):
-    return [(a, b) for a in range(n) for b in range(a, n)]
+    return [(a, b) for a in range(n) for b in range(a + 1, n)]
+
+
+def packed_rows(n):
+    return len(pairs(n)) * HALF + n // 2 * HALF + n % 2 * (HALF // 2)
+
+
+def halves_of(block):
+    low = lanes_of(block) < HALF
+    row = lax.broadcasted_iota(jnp.int32, block.shape, 0)
+    col = jnp.where(low, lanes_of(block), lanes_of(block) - HALF)
+    return low, row, col
+
+
+def hermitian_low(block):
+    _, row, col = halves_of(block)
+    return jnp.where(row <= col, block, pltpu.roll(block, HALF, 1))
+
+
+def hermitian_high(block):
+    _, row, col = halves_of(block)
+    return jnp.where(row <= col, pltpu.roll(block, HALF, 1), block)
 
 
 def packed(z):
     n = z.shape[0] // HALF
-    return jnp.concatenate(
-        [z[a * HALF : (a + 1) * HALF, b * LANES : (b + 1) * LANES] for a, b in pairs(n)], axis=0
-    )
+
+    def block(a, b):
+        return z[a * HALF : (a + 1) * HALF, b * LANES : (b + 1) * LANES]
+
+    parts = [block(a, b) for a, b in pairs(n)]
+    for a in range(0, n - 1, 2):
+        first, second = hermitian_low(block(a, a)), hermitian_high(block(a + 1, a + 1))
+        parts.append(jnp.where(lanes_of(first) < HALF, first, second))
+    if n % 2:
+        last = hermitian_low(block(n - 1, n - 1))
+        top, bottom = last[: HALF // 2], pltpu.roll(last[HALF // 2 :], HALF, 1)
+        parts.append(jnp.where(lanes_of(top) < HALF, top, bottom))
+    return jnp.concatenate(parts, axis=0)
+
+
+def hermitian(half):
+    low, row, col = halves_of(half)
+    twice = jnp.where(low, half, pltpu.roll(half, HALF, 1))
+    t = twice.T
+    flipped = jnp.concatenate([t[:HALF], t[HALF:]], axis=1)
+    re = jnp.where(row <= col, twice, flipped)
+    im = jnp.where(row > col, twice, jnp.where(row < col, -flipped, 0.0))
+    return jnp.where(low, re, im)
 
 
 def adjoint(block):
@@ -81,11 +122,23 @@
 
 def unpack_to(ref, p):
     n = ref.shape[0] // HALF
+
+    def put(a, b, block):
+        ref[a * HALF : (a + 1) * HALF, b * LANES : (b + 1) * LANES] = block
+
     for k, (a, b) in enumerate(pairs(n)):
         block = p[k * HALF : (k + 1) * HALF]
-        ref[a * HALF : (a + 1) * HALF, b * LANES : (b + 1) * LANES] = block
-        if a != b:
-            ref[b * HALF : (b + 1) * HALF, a * LANES : (a + 1) * LANES] = adjoint(block)
+        put(a, b, block)
+        put(b, a, adjoint(block))
+    start = len(pairs(n)) * HALF
+    for a in range(0, n - 1, 2):
+        block = p[start : start + HALF]
+        put(a, a, hermitian(block))
+        put(a + 1, a + 1, hermitian(pltpu.roll(block, HALF, 1)))
+        start += HALF
+    if n % 2:
+        block = p[start : start + HALF // 2]
+        put(n - 1, n - 1, hermitian(jnp.concatenate([block, pltpu.roll(block, HALF, 1)], axis=0)))
 
 
 def lane_copy(x, lane):
@@ -358,7 +411,7 @@
     order, width = couplings.shape[1:]
     cols = sources.shape[1]
     nb = order // HALF
-    size = len(pairs(nb)) * HALF
+    size = packed_rows(nb)
     whole = f32(order, width)
     vv_shape = f32(size, LANES)
     sides = (

time: 173 us -> 171 us (0.988)
  waiting for transfers between devices: 26.1 us -> 22.2 us
  Pallas kernels: 81.8 us -> 84.1 us
    ppermute x8, waiting for transfers between devices: 12 us -> 8.05 us  [forward_to(): lax.ppermute(x, axis, [(i + distance, i) for i in range(0, n, 2 * distanc...]
    pallas_call x14, Pallas kernels: 81.8 us -> 84.1 us  [run(): pl.pallas_call(kernel, out_shape=outs, in_specs=specs, out_specs=jax.tree...]
  transfers between devices with their start and end apart: 14 -> 14, of which waited for: 12 -> 11; matrix products, arithmetic and copies ran while one was open for 0% -> 0% of each run, Pallas kernels for 40% -> 42%
where the time goes in v2:
time: 171 us
  Pallas kernels  84.1 us (49%)
  starting transfers between devices  60.7 us (35%)
  waiting for transfers between devices  22.2 us (13%)
  blocking collectives  2.25 us (1%)
    pallas_call x14, Pallas kernels, run(): pl.pallas_call(kernel, out_shape=outs, in_specs=specs, out_specs=jax.tree...  84.1 us
    all_to_all x1, starting transfers between devices, gathered(): lax.all_to_all(copies, 'orb', split_axis=0, concat_axis=0, tiled=True)  43.7 us
    ppermute x8, starting transfers between devices, forward_to(): lax.ppermute(x, axis, [(i + distance, i) for i in range(0, n, 2 * distanc...  10.4 us
    all_to_all x1, waiting for transfers between devices, gathered(): lax.all_to_all(copies, 'orb', split_axis=0, concat_axis=0, tiled=True)  8.11 us
    ppermute x8, waiting for transfers between devices, forward_to(): lax.ppermute(x, axis, [(i + distance, i) for i in range(0, n, 2 * distanc...  8.05 us
    ppermute x4, waiting for transfers between devices, back_to(): lax.ppermute(x, axis, [(i, i + distance) for i in range(0, n, 2 * distanc...  6.01 us
    ppermute x4, starting transfers between devices, back_to(): lax.ppermute(x, axis, [(i, i + distance) for i in range(0, n, 2 * distanc...  5.24 us
  transfers between devices with their start and end apart: 14, of which 11 were waited for; matrix products, arithmetic and copies ran while one was open for 0% of the time, Pallas kernels for 42%

profile of v2, /device:TPU:66, one launch (start us, length us, event | category | flops | bytes accessed | tf_op | source)
XLA Modules:
  0.0 171.0 jit_solution(14130157076613678458)
XLA Ops:
  0.0 0.0 copy-start
  0.0 0.9 select_bitcast_fusion
  0.9 0.7 broadcast_in_dim.4
  1.6 43.7 %all-to-all-start = ((f32[8,24,384]{2,1,0:T(8,128)}), f32[8,24,384]{2,1,0:T(8,128)S(1)}, u32[]{:S(2)}, u32[]{:S(2)}) async-start(f32[8,24,384]{2,1,0:T(8,128)} %broadcast_in_dim.4), calls=%async_computation | async-start | bytes 589824 | tf_op jit(solution)/shard_map/all_to_all | solution.py:406
  45.3 0.0 copy-done
  45.4 1.3 collective-permute-start.1
  46.7 8.1 %all-to-all-done = f32[8,24,384]{2,1,0:T(8,128)S(1)} async-done(((f32[8,24,384]{2,1,0:T(8,128)}), f32[8,24,384]{2,1,0:T(8,128)S(1)}, u32[]{:S(2)}, u32[]{:S(2)}) %all-to-all-start) | async-done | bytes 294944 | tf_op jit(solution)/shard_map/all_to_all | solution.py:406
  54.8 2.2 %all_gather.3.diag_ref = f32[2,192,384]{2,1,0:T(8,128)S(1)} all-gather(f32[1,192,384]{2,1,0:T(8,128)S(1)} %bitcast.6), channel_id=1, replica_groups=mesh['energy'=2,'slab'=16,'orb'=8,'rhs'=2] {'rhs'}, dimensions={0}, use_global_device_ids=true | all-gather | bytes 884736 | tf_op jit(solution)/shard_map/all_gather | solution.py:407
  57.0 10.6 %shard_map.37 = (f32[192,384]{1,0:T(8,128)S(1)}, f32[192,384]{1,0:T(8,128)S(1)}, f32[288,128]{1,0:T(8,128)S(1)}) custom-call(f32[2,192,384]{2,1,0:T(8,128)S(1)} %all_gather.3.diag_ref, f32[2,192,384]{2,1,0:T(8,128)S(1)} %copy-done), custom_call_target="tpu_custom_call" | custom-call | flops 4000000000 | bytes 1000000 | tf_op jit(solution)/shard_map/pallas_call | solution.py:381
  67.6 1.3 collective-permute-start
  68.9 0.0 collective-permute-done.1.next_ref
  69.0 0.0 copy-done.1
  69.0 4.3 %shard_map.38 = (f32[912,128]{1,0:T(8,128)S(1)}, f32[16,384]{1,0:T(8,128)}, f32[8,384]{1,0:T(8,128)S(1)}, f32[384,384]{1,0:T(8,128)S(1)}) custom-call(f32[2,192,384]{2,1,0:T(8,128)S(1)} %copy-done, f32[192,384]{1,0:T(8,128)S(1)} %collective-permute-done.1.next_ref, f32[2,8,384]{2,1,0:T(8,128)S(1)} %copy-done.1, f32[192,384]{1,0:T(8,128)S(1)} %get-tuple-element.43.w_ref, ...), custom_call_target="tpu_custom_call" | custom-call | flops 1000000000 | bytes 1000000 | tf_op jit(solution)/shard_map/pallas_call | solution.py:381
  73.3 1.3 collective-permute-start.3
  74.6 0.8 collective-permute-done.refs_0_
  75.4 11.0 %shard_map.39 = (f32[192,384]{1,0:T(8,128)S(1)}, f32[192,384]{1,0:T(8,128)S(1)}, f32[288,128]{1,0:T(8,128)S(1)}) custom-call(s32[1]{0:T(128)} %bitcast.slab_ref, f32[288,128]{1,0:T(8,128)S(1)} %collective-permute-done.refs_0_, f32[288,128]{1,0:T(8,128)S(1)} %get-tuple-element.42.refs_1_, f32[912,128]{1,0:T(8,128)S(1)} %get-tuple-element.45.refs_2_), custom_call_target="tpu_custom_call" | custom-call | flops 4000000000 | bytes 1000000 | tf_op jit(solution)/shard_map/pallas_call | solution.py:381
  86.5 1.3 collective-permute-start.2
  87.8 0.2 collective-permute-done.3.refs_3_
  87.9 4.2 %shard_map.40 = (f32[912,128]{1,0:T(8,128)S(1)}, f32[16,384]{1,0:T(8,128)}, f32[8,384]{1,0:T(8,128)S(1)}, f32[384,384]{1,0:T(8,128)S(1)}) custom-call(s32[1]{0:T(128)} %bitcast.slab_ref, f32[192,384]{1,0:T(8,128)S(1)} %get-tuple-element.47.refs_0_, f32[192,384]{1,0:T(8,128)S(1)} %get-tuple-element.48.refs_1_, f32[912,128]{1,0:T(8,128)S(1)} %get-tuple-element.45.refs_2_, ...), custom_call_target="tpu_custom_call" | custom-call | flops 1000000000 | bytes 1000000 | tf_op jit(solution)/shard_map/pallas_call | solution.py:381
  92.2 1.3 collective-permute-start.5
  93.5 1.0 collective-permute-done.2.refs_0_
  94.4 11.0 %shard_map.41 = (f32[192,384]{1,0:T(8,128)S(1)}, f32[192,384]{1,0:T(8,128)S(1)}, f32[288,128]{1,0:T(8,128)S(1)}) custom-call(s32[1]{0:T(128)} %bitcast.slab_ref, f32[288,128]{1,0:T(8,128)S(1)} %collective-permute-done.2.refs_0_, f32[288,128]{1,0:T(8,128)S(1)} %get-tuple-element.46.refs_1_, f32[912,128]{1,0:T(8,128)S(1)} %get-tuple-element.49.refs_2_), custom_call_target="tpu_custom_call" | custom-call | flops 4000000000 | bytes 1000000 | tf_op jit(solution)/shard_map/pallas_call | solution.py:381
  105.4 1.3 collective-permute-start.4
  106.8 0.1 collective-permute-done.5.refs_3_
  106.9 4.2 %shard_map.42 = (f32[912,128]{1,0:T(8,128)S(1)}, f32[16,384]{1,0:T(8,128)}, f32[8,384]{1,0:T(8,128)S(1)}, f32[384,384]{1,0:T(8,128)S(1)}) custom-call(s32[1]{0:T(128)} %bitcast.slab_ref, f32[192,384]{1,0:T(8,128)S(1)} %get-tuple-element.51.refs_0_, f32[192,384]{1,0:T(8,128)S(1)} %get-tuple-element.52.refs_1_, f32[912,128]{1,0:T(8,128)S(1)} %get-tuple-element.49.refs_2_, ...), custom_call_target="tpu_custom_call" | custom-call | flops 1000000000 | bytes 1000000 | tf_op jit(solution)/shard_map/pallas_call | solution.py:381
  111.1 1.3 collective-permute-start.7
  112.4 4.0 %collective-permute-done.4.refs_0_ = f32[288,128]{1,0:T(8,128)S(1)} collective-permute-done((f32[288,128]{1,0:T(8,128)S(1)}, f32[288,128]{1,0:T(8,128)S(1)}, u32[]{:S(2)}, u32[]{:S(2)}) %collective-permute-start.4) | collective-permute-done | bytes 147488 | tf_op jit(solution)/shard_map/ppermute | solution.py:394
  116.4 11.0 %shard_map.43 = (f32[192,384]{1,0:T(8,128)S(1)}, f32[192,384]{1,0:T(8,128)S(1)}, f32[288,128]{1,0:T(8,128)S(1)}) custom-call(s32[1]{0:T(128)} %bitcast.slab_ref, f32[288,128]{1,0:T(8,128)S(1)} %collective-permute-done.4.refs_0_, f32[288,128]{1,0:T(8,128)S(1)} %get-tuple-element.50.refs_1_, f32[912,128]{1,0:T(8,128)S(1)} %get-tuple-element.53.refs_2_), custom_call_target="tpu_custom_call" | custom-call | flops 4000000000 | bytes 1000000 | tf_op jit(solution)/shard_map/pallas_call | solution.py:381
  127.4 1.3 collective-permute-start.6
  128.7 0.0 collective-permute-done.7.refs_3_
  128.8 3.8 %shard_map.44 = (f32[912,128]{1,0:T(8,128)S(1)}, f32[16,384]{1,0:T(8,128)S(1)}, f32[8,384]{1,0:T(8,128)S(1)}, f32[384,384]{1,0:T(8,128)S(1)}) custom-call(s32[1]{0:T(128)} %bitcast.slab_ref, f32[192,384]{1,0:T(8,128)S(1)} %get-tuple-element.55.refs_0_, f32[192,384]{1,0:T(8,128)S(1)} %get-tuple-element.56.refs_1_, f32[912,128]{1,0:T(8,128)S(1)} %get-tuple-element.53.refs_2_, ...), custom_call_target="tpu_custom_call" | custom-call | flops 1000000000 | bytes 1000000 | tf_op jit(solution)/shard_map/pallas_call | solution.py:381
  132.6 1.3 collective-permute-start.8
  133.9 11.2 %shard_map.45 = (f32[288,128]{1,0:T(8,128)S(1)}, f32[192,384]{1,0:T(8,128)S(1)}, f32[8,384]{1,0:T(8,128)S(1)}, f32[8,384]{1,0:T(8,128)S(1)}) custom-call(s32[1]{0:T(128)} %bitcast.slab_ref, f32[288,128]{1,0:T(8,128)S(1)} %get-tuple-element.54.refs_0_, f32[912,128]{1,0:T(8,128)S(1)} %get-tuple-element.58.refs_1_, f32[16,384]{1,0:T(8,128)S(1)} %get-tuple-element.57.refs_2_), custom_call_target="tpu_custom_call" | custom-call | flops 4000000000 | bytes 1000000 | tf_op jit(solution)/shard_map/pallas_call | solution.py:381
  145.1 0.0 collective-permute-done.6.refs_0_
  145.1 1.9 %collective-permute-done.8.refs_1_ = f32[16,384]{1,0:T(8,128)S(1)} collective-permute-done((f32[16,384]{1,0:T(8,128)S(1)}, f32[16,384]{1,0:T(8,128)S(1)}, u32[]{:S(2)}, u32[]{:S(2)}) %collective-permute-start.8) | collective-permute-done | bytes 24608 | tf_op jit(solution)/shard_map/ppermute | solution.py:394
  147.0 10.1 %shard_map.46 = (f32[16,384]{1,0:T(8,128)S(1)}, f32[8,384]{1,0:T(8,128)S(1)}) custom-call(s32[1]{0:T(128)} %bitcast.slab_ref, f32[288,128]{1,0:T(8,128)S(1)} %collective-permute-done.6.refs_0_, f32[16,384]{1,0:T(8,128)S(1)} %collective-permute-done.8.refs_1_, f32[288,128]{1,0:T(8,128)S(1)} %get-tuple-element.59.refs_2_, ...), custom_call_target="tpu_custom_call" | custom-call | flops 4000000000 | bytes 1000000 | tf_op jit(solution)/shard_map/pallas_call | solution.py:381
  157.1 1.3 collective-permute-start.9
  158.5 1.5 collective-permute-done.9.got_ref
  160.0 0.5 shard_map.47
  160.4 1.3 collective-permute-start.10
  161.8 1.5 collective-permute-done.10.got_ref
  163.3 0.5 shard_map.48
  163.7 1.3 collective-permute-start.11
  165.0 1.5 collective-permute-done.11.got_ref
  166.6 0.5 shard_map.49
  167.0 1.3 collective-permute-start.12
  168.3 1.5 collective-permute-done.12.got_ref
  169.8 1.2 shard_map.50
  (2 shorter events, 0.0 us)
Async XLA Ops:
  0.0 45.3 %copy-start = (f32[2,192,384]{2,1,0:T(8,128)S(1)}, f32[2,192,384]{2,1,0:T(8,128)}, u32[]{:S(2)}) copy-start(f32[2,192,384]{2,1,0:T(8,128)} %coup_ref.3) | copy-start | bytes 1769476
  1.6 53.2 %all-to-all-start = ((f32[8,24,384]{2,1,0:T(8,128)}), f32[8,24,384]{2,1,0:T(8,128)S(1)}, u32[]{:S(2)}, u32[]{:S(2)}) async-start(f32[8,24,384]{2,1,0:T(8,128)} %broadcast_in_dim.4), calls=%async_computation | async-start | bytes 589824 | tf_op jit(solution)/shard_map/all_to_all | solution.py:406
  45.4 23.6 %collective-permute-start.1 = (f32[192,384]{1,0:T(8,128)S(1)}, f32[192,384]{1,0:T(8,128)S(1)}, u32[]{:S(2)}, u32[]{:S(2)}) collective-permute-start(f32[192,384]{1,0:T(8,128)S(1)} %slice_bitcast_fusion), channel_id=1, source_target_pairs={{16,0},{32,16},{48,32},{64,48},{80,64},{96,80},{112,96},{128,112},... | collective-permute-start | bytes 884744 | tf_op jit(solution)/shard_map/ppermute | solution.py:426
  57.0 11.9 %copy-start.1 = (f32[2,8,384]{2,1,0:T(8,128)S(1)}, f32[2,8,384]{2,1,0:T(8,128)}, u32[]{:S(2)}) copy-start(f32[2,8,384]{2,1,0:T(8,128)} %src_ref.1) | copy-start | bytes 73732
  67.6 7.8 %collective-permute-start = (f32[288,128]{1,0:T(8,128)S(1)}, f32[288,128]{1,0:T(8,128)S(1)}, u32[]{:S(2)}, u32[]{:S(2)}) collective-permute-start(f32[288,128]{1,0:T(8,128)S(1)} %get-tuple-element.42.refs_1_), channel_id=1, source_target_pairs={{16,0},{48,32},{80,64},{112,96},{144,128},{176,160},{208,192},{240... | collective-permute-start | bytes 442376 | tf_op jit(solution)/shard_map/ppermute | solution.py:394
  73.3 14.6 %collective-permute-start.3 = (f32[912,128]{1,0:T(8,128)S(1)}, f32[912,128]{1,0:T(8,128)S(1)}, u32[]{:S(2)}, u32[]{:S(2)}) collective-permute-start(f32[912,128]{1,0:T(8,128)S(1)} %get-tuple-element.45.refs_2_), channel_id=1, source_target_pairs={{16,0},{48,32},{80,64},{112,96},{144,128},{176,160},{208,192},{240... | collective-permute-start | bytes 1400840 | tf_op jit(solution)/shard_map/ppermute | solution.py:394
  86.5 8.0 %collective-permute-start.2 = (f32[288,128]{1,0:T(8,128)S(1)}, f32[288,128]{1,0:T(8,128)S(1)}, u32[]{:S(2)}, u32[]{:S(2)}) collective-permute-start(f32[288,128]{1,0:T(8,128)S(1)} %get-tuple-element.46.refs_1_), channel_id=1, source_target_pairs={{32,0},{96,64},{160,128},{224,192},{33,1},{97,65},{161,129},{225,1... | collective-permute-start | bytes 442376 | tf_op jit(solution)/shard_map/ppermute | solution.py:394
  92.2 14.7 %collective-permute-start.5 = (f32[912,128]{1,0:T(8,128)S(1)}, f32[912,128]{1,0:T(8,128)S(1)}, u32[]{:S(2)}, u32[]{:S(2)}) collective-permute-start(f32[912,128]{1,0:T(8,128)S(1)} %get-tuple-element.49.refs_2_), channel_id=1, source_target_pairs={{32,0},{96,64},{160,128},{224,192},{33,1},{97,65},{161,129},{225,1... | collective-permute-start | bytes 1400840 | tf_op jit(solution)/shard_map/ppermute | solution.py:394
  105.4 11.0 %collective-permute-start.4 = (f32[288,128]{1,0:T(8,128)S(1)}, f32[288,128]{1,0:T(8,128)S(1)}, u32[]{:S(2)}, u32[]{:S(2)}) collective-permute-start(f32[288,128]{1,0:T(8,128)S(1)} %get-tuple-element.50.refs_1_), channel_id=1, source_target_pairs={{64,0},{192,128},{65,1},{193,129},{66,2},{194,130},{67,3},{195,131... | collective-permute-start | bytes 442376 | tf_op jit(solution)/shard_map/ppermute | solution.py:394
  111.1 17.7 %collective-permute-start.7 = (f32[912,128]{1,0:T(8,128)S(1)}, f32[912,128]{1,0:T(8,128)S(1)}, u32[]{:S(2)}, u32[]{:S(2)}) collective-permute-start(f32[912,128]{1,0:T(8,128)S(1)} %get-tuple-element.53.refs_2_), channel_id=1, source_target_pairs={{64,0},{192,128},{65,1},{193,129},{66,2},{194,130},{67,3},{195,131... | collective-permute-start | bytes 1400840 | tf_op jit(solution)/shard_map/ppermute | solution.py:394
  127.4 17.7 %collective-permute-start.6 = (f32[288,128]{1,0:T(8,128)S(1)}, f32[288,128]{1,0:T(8,128)S(1)}, u32[]{:S(2)}, u32[]{:S(2)}) collective-permute-start(f32[288,128]{1,0:T(8,128)S(1)} %get-tuple-element.54.refs_0_), channel_id=1, source_target_pairs={{128,0},{129,1},{130,2},{131,3},{132,4},{133,5},{134,6},{135,7},{1... | collective-permute-start | bytes 442376 | tf_op jit(solution)/shard_map/ppermute | solution.py:394
  132.6 14.5 %collective-permute-start.8 = (f32[16,384]{1,0:T(8,128)S(1)}, f32[16,384]{1,0:T(8,128)S(1)}, u32[]{:S(2)}, u32[]{:S(2)}) collective-permute-start(f32[16,384]{1,0:T(8,128)S(1)} %get-tuple-element.57.refs_2_), channel_id=1, source_target_pairs={{128,0},{129,1},{130,2},{131,3},{132,4},{133,5},{134,6},{135,7},{1... | collective-permute-start | bytes 73736 | tf_op jit(solution)/shard_map/ppermute | solution.py:394
  157.1 2.8 %collective-permute-start.9 = (f32[16,384]{1,0:T(8,128)S(1)}, f32[16,384]{1,0:T(8,128)S(1)}, u32[]{:S(2)}, u32[]{:S(2)}) collective-permute-start(f32[16,384]{1,0:T(8,128)S(1)} %get-tuple-element.63.prev_ref), channel_id=1, source_target_pairs={{0,128},{1,129},{2,130},{3,131},{4,132},{5,133},{6,134},{7,135},{8... | collective-permute-start | bytes 73736 | tf_op jit(solution)/shard_map/ppermute | solution.py:399
  160.4 2.8 %collective-permute-start.10 = (f32[16,384]{1,0:T(8,128)S(1)}, f32[16,384]{1,0:T(8,128)S(1)}, u32[]{:S(2)}, u32[]{:S(2)}) collective-permute-start(f32[16,384]{1,0:T(8,128)S(1)} %get-tuple-element.67.prev_ref), channel_id=1, source_target_pairs={{0,64},{128,192},{1,65},{129,193},{2,66},{130,194},{3,67},{131,195... | collective-permute-start | bytes 73736 | tf_op jit(solution)/shard_map/ppermute | solution.py:399
  163.7 2.8 %collective-permute-start.11 = (f32[16,384]{1,0:T(8,128)S(1)}, f32[16,384]{1,0:T(8,128)S(1)}, u32[]{:S(2)}, u32[]{:S(2)}) collective-permute-start(f32[16,384]{1,0:T(8,128)S(1)} %get-tuple-element.71.prev_ref), channel_id=1, source_target_pairs={{0,32},{64,96},{128,160},{192,224},{1,33},{65,97},{129,161},{193,2... | collective-permute-start | bytes 73736 | tf_op jit(solution)/shard_map/ppermute | solution.py:399
  167.0 2.8 %collective-permute-start.12 = (f32[16,384]{1,0:T(8,128)S(1)}, f32[16,384]{1,0:T(8,128)S(1)}, u32[]{:S(2)}, u32[]{:S(2)}) collective-permute-start(f32[16,384]{1,0:T(8,128)S(1)} %get-tuple-element.75.prev_ref), channel_id=1, source_target_pairs={{0,16},{32,48},{64,80},{96,112},{128,144},{160,176},{192,208},{224... | collective-permute-start | bytes 73736 | tf_op jit(solution)/shard_map/ppermute | solution.py:399

commit v3 on v2

--- a/solution.py
+++ b/solution.py
@@ -399,12 +399,18 @@
     return lax.ppermute(x, axis, [(i, i + distance) for i in range(0, n, 2 * distance)])
 
 
+def copies_kernel(which_ref, diag_ref, out_ref):
+    mine = jnp.where(which_ref[0] == 0, diag_ref[0], diag_ref[1])
+    for k in range(out_ref.shape[0]):
+        out_ref[k] = mine
+
+
 def gathered(diag_blocks):
-    width = diag_blocks.shape[2]
-    copies = [jnp.broadcast_to(layer, (lax.axis_size("orb"), *layer.shape)) for layer in diag_blocks]
-    copies = jnp.where(lax.axis_index("rhs") == 0, copies[0], copies[1])
+    which = lax.axis_index("rhs").astype(jnp.int32).reshape(1)
+    shape = (lax.axis_size("orb"), *diag_blocks.shape[1:])
+    copies = run(copies_kernel, f32(*shape), which, diag_blocks, scalars=1, flops=10**6)
     whole = lax.all_to_all(copies, "orb", split_axis=0, concat_axis=0, tiled=True)
-    return lax.all_gather(whole.reshape(-1, width), "rhs")
+    return lax.all_gather(whole.reshape(-1, shape[2]), "rhs")
 
 
 def local(diag_blocks, couplings, sources):

time: 171 us -> 172 us (level)
    pallas_call x14 -> x15, Pallas kernels: 84.1 us -> 84.8 us  [run(): pl.pallas_call(kernel, out_shape=outs, in_specs=specs, out_specs=jax.tree...]
where the time goes in v3:
time: 172 us; the launch traced here: 171 us
  Pallas kernels  84.8 us (49%)
  starting transfers between devices  60.7 us (35%)
  waiting for transfers between devices  22.2 us (13%)
  blocking collectives  2.25 us (1%)
    pallas_call x15, Pallas kernels, run(): pl.pallas_call(kernel, out_shape=outs, in_specs=specs, out_specs=jax.tree...  84.8 us
    all_to_all x1, starting transfers between devices, gathered(): lax.all_to_all(copies, 'orb', split_axis=0, concat_axis=0, tiled=True)  43.7 us
    ppermute x8, starting transfers between devices, forward_to(): lax.ppermute(x, axis, [(i + distance, i) for i in range(0, n, 2 * distanc...  10.4 us
    all_to_all x1, waiting for transfers between devices, gathered(): lax.all_to_all(copies, 'orb', split_axis=0, concat_axis=0, tiled=True)  8.11 us
    ppermute x8, waiting for transfers between devices, forward_to(): lax.ppermute(x, axis, [(i + distance, i) for i in range(0, n, 2 * distanc...  8.07 us
    ppermute x4, waiting for transfers between devices, back_to(): lax.ppermute(x, axis, [(i, i + distance) for i in range(0, n, 2 * distanc...  6.01 us
    ppermute x4, starting transfers between devices, back_to(): lax.ppermute(x, axis, [(i, i + distance) for i in range(0, n, 2 * distanc...  5.24 us
  transfers between devices with their start and end apart: 14, of which 11 were waited for; matrix products, arithmetic and copies ran while one was open for 0% of the time, Pallas kernels for 42%

profile of v3, /device:TPU:66, one launch (start us, length us, event | category | flops | bytes accessed | tf_op | source)
XLA Modules:
  0.0 171.1 jit_solution(7208470514167742525)
XLA Ops:
  0.0 0.0 copy-start
  0.0 0.9 copy-done.1
  0.9 0.7 shard_map.37
  1.7 43.7 %all-to-all-start = ((f32[8,24,384]{2,1,0:T(8,128)}), f32[8,24,384]{2,1,0:T(8,128)S(1)}, u32[]{:S(2)}, u32[]{:S(2)}) async-start(f32[8,24,384]{2,1,0:T(8,128)} %shard_map.37), calls=%async_computation | async-start | bytes 589824 | tf_op jit(solution)/shard_map/all_to_all | solution.py:412
  45.4 0.0 copy-done
  45.4 1.3 collective-permute-start.1
  46.8 8.1 %all-to-all-done = f32[8,24,384]{2,1,0:T(8,128)S(1)} async-done(((f32[8,24,384]{2,1,0:T(8,128)}), f32[8,24,384]{2,1,0:T(8,128)S(1)}, u32[]{:S(2)}, u32[]{:S(2)}) %all-to-all-start) | async-done | bytes 294944 | tf_op jit(solution)/shard_map/all_to_all | solution.py:412
  54.9 2.2 %all_gather.3.diag_ref = f32[2,192,384]{2,1,0:T(8,128)S(1)} all-gather(f32[1,192,384]{2,1,0:T(8,128)S(1)} %bitcast.5), channel_id=1, replica_groups=mesh['energy'=2,'slab'=16,'orb'=8,'rhs'=2] {'rhs'}, dimensions={0}, use_global_device_ids=true | all-gather | bytes 884736 | tf_op jit(solution)/shard_map/all_gather | solution.py:413
  57.1 10.6 %shard_map.38 = (f32[192,384]{1,0:T(8,128)S(1)}, f32[192,384]{1,0:T(8,128)S(1)}, f32[288,128]{1,0:T(8,128)S(1)}) custom-call(f32[2,192,384]{2,1,0:T(8,128)S(1)} %all_gather.3.diag_ref, f32[2,192,384]{2,1,0:T(8,128)S(1)} %copy-done), custom_call_target="tpu_custom_call" | custom-call | flops 4000000000 | bytes 1000000 | tf_op jit(solution)/shard_map/pallas_call | solution.py:381
  67.7 1.3 collective-permute-start
  69.0 0.0 collective-permute-done.1.next_ref
  69.0 0.0 copy-done.2
  69.0 4.3 %shard_map.39 = (f32[912,128]{1,0:T(8,128)S(1)}, f32[16,384]{1,0:T(8,128)}, f32[8,384]{1,0:T(8,128)S(1)}, f32[384,384]{1,0:T(8,128)S(1)}) custom-call(f32[2,192,384]{2,1,0:T(8,128)S(1)} %copy-done, f32[192,384]{1,0:T(8,128)S(1)} %collective-permute-done.1.next_ref, f32[2,8,384]{2,1,0:T(8,128)S(1)} %copy-done.2, f32[192,384]{1,0:T(8,128)S(1)} %get-tuple-element.43.w_ref, ...), custom_call_target="tpu_custom_call" | custom-call | flops 1000000000 | bytes 1000000 | tf_op jit(solution)/shard_map/pallas_call | solution.py:381
  73.3 1.3 collective-permute-start.3
  74.7 0.9 collective-permute-done.refs_0_
  75.5 11.0 %shard_map.40 = (f32[192,384]{1,0:T(8,128)S(1)}, f32[192,384]{1,0:T(8,128)S(1)}, f32[288,128]{1,0:T(8,128)S(1)}) custom-call(s32[1]{0:T(128)} %bitcast.slab_ref, f32[288,128]{1,0:T(8,128)S(1)} %collective-permute-done.refs_0_, f32[288,128]{1,0:T(8,128)S(1)} %get-tuple-element.42.refs_1_, f32[912,128]{1,0:T(8,128)S(1)} %get-tuple-element.45.refs_2_), custom_call_target="tpu_custom_call" | custom-call | flops 4000000000 | bytes 1000000 | tf_op jit(solution)/shard_map/pallas_call | solution.py:381
  86.5 1.3 collective-permute-start.2
  87.9 0.2 collective-permute-done.3.refs_3_
  88.0 4.2 %shard_map.41 = (f32[912,128]{1,0:T(8,128)S(1)}, f32[16,384]{1,0:T(8,128)}, f32[8,384]{1,0:T(8,128)S(1)}, f32[384,384]{1,0:T(8,128)S(1)}) custom-call(s32[1]{0:T(128)} %bitcast.slab_ref, f32[192,384]{1,0:T(8,128)S(1)} %get-tuple-element.47.refs_0_, f32[192,384]{1,0:T(8,128)S(1)} %get-tuple-element.48.refs_1_, f32[912,128]{1,0:T(8,128)S(1)} %get-tuple-element.45.refs_2_, ...), custom_call_target="tpu_custom_call" | custom-call | flops 1000000000 | bytes 1000000 | tf_op jit(solution)/shard_map/pallas_call | solution.py:381
  92.2 1.3 collective-permute-start.5
  93.5 1.0 collective-permute-done.2.refs_0_
  94.5 11.0 %shard_map.42 = (f32[192,384]{1,0:T(8,128)S(1)}, f32[192,384]{1,0:T(8,128)S(1)}, f32[288,128]{1,0:T(8,128)S(1)}) custom-call(s32[1]{0:T(128)} %bitcast.slab_ref, f32[288,128]{1,0:T(8,128)S(1)} %collective-permute-done.2.refs_0_, f32[288,128]{1,0:T(8,128)S(1)} %get-tuple-element.46.refs_1_, f32[912,128]{1,0:T(8,128)S(1)} %get-tuple-element.49.refs_2_), custom_call_target="tpu_custom_call" | custom-call | flops 4000000000 | bytes 1000000 | tf_op jit(solution)/shard_map/pallas_call | solution.py:381
  105.5 1.3 collective-permute-start.4
  106.8 0.1 collective-permute-done.5.refs_3_
  107.0 4.2 %shard_map.43 = (f32[912,128]{1,0:T(8,128)S(1)}, f32[16,384]{1,0:T(8,128)}, f32[8,384]{1,0:T(8,128)S(1)}, f32[384,384]{1,0:T(8,128)S(1)}) custom-call(s32[1]{0:T(128)} %bitcast.slab_ref, f32[192,384]{1,0:T(8,128)S(1)} %get-tuple-element.51.refs_0_, f32[192,384]{1,0:T(8,128)S(1)} %get-tuple-element.52.refs_1_, f32[912,128]{1,0:T(8,128)S(1)} %get-tuple-element.49.refs_2_, ...), custom_call_target="tpu_custom_call" | custom-call | flops 1000000000 | bytes 1000000 | tf_op jit(solution)/shard_map/pallas_call | solution.py:381
  111.2 1.3 collective-permute-start.7
  112.5 4.0 %collective-permute-done.4.refs_0_ = f32[288,128]{1,0:T(8,128)S(1)} collective-permute-done((f32[288,128]{1,0:T(8,128)S(1)}, f32[288,128]{1,0:T(8,128)S(1)}, u32[]{:S(2)}, u32[]{:S(2)}) %collective-permute-start.4) | collective-permute-done | bytes 147488 | tf_op jit(solution)/shard_map/ppermute | solution.py:394
  116.5 11.0 %shard_map.44 = (f32[192,384]{1,0:T(8,128)S(1)}, f32[192,384]{1,0:T(8,128)S(1)}, f32[288,128]{1,0:T(8,128)S(1)}) custom-call(s32[1]{0:T(128)} %bitcast.slab_ref, f32[288,128]{1,0:T(8,128)S(1)} %collective-permute-done.4.refs_0_, f32[288,128]{1,0:T(8,128)S(1)} %get-tuple-element.50.refs_1_, f32[912,128]{1,0:T(8,128)S(1)} %get-tuple-element.53.refs_2_), custom_call_target="tpu_custom_call" | custom-call | flops 4000000000 | bytes 1000000 | tf_op jit(solution)/shard_map/pallas_call | solution.py:381
  127.5 1.3 collective-permute-start.6
  128.8 0.0 collective-permute-done.7.refs_3_
  128.8 3.8 %shard_map.45 = (f32[912,128]{1,0:T(8,128)S(1)}, f32[16,384]{1,0:T(8,128)S(1)}, f32[8,384]{1,0:T(8,128)S(1)}, f32[384,384]{1,0:T(8,128)S(1)}) custom-call(s32[1]{0:T(128)} %bitcast.slab_ref, f32[192,384]{1,0:T(8,128)S(1)} %get-tuple-element.55.refs_0_, f32[192,384]{1,0:T(8,128)S(1)} %get-tuple-element.56.refs_1_, f32[912,128]{1,0:T(8,128)S(1)} %get-tuple-element.53.refs_2_, ...), custom_call_target="tpu_custom_call" | custom-call | flops 1000000000 | bytes 1000000 | tf_op jit(solution)/shard_map/pallas_call | solution.py:381
  132.6 1.3 collective-permute-start.8
  134.0 11.2 %shard_map.46 = (f32[288,128]{1,0:T(8,128)S(1)}, f32[192,384]{1,0:T(8,128)S(1)}, f32[8,384]{1,0:T(8,128)S(1)}, f32[8,384]{1,0:T(8,128)S(1)}) custom-call(s32[1]{0:T(128)} %bitcast.slab_ref, f32[288,128]{1,0:T(8,128)S(1)} %get-tuple-element.54.refs_0_, f32[912,128]{1,0:T(8,128)S(1)} %get-tuple-element.58.refs_1_, f32[16,384]{1,0:T(8,128)S(1)} %get-tuple-element.57.refs_2_), custom_call_target="tpu_custom_call" | custom-call | flops 4000000000 | bytes 1000000 | tf_op jit(solution)/shard_map/pallas_call | solution.py:381
  145.2 0.0 collective-permute-done.6.refs_0_
  145.2 1.9 %collective-permute-done.8.refs_1_ = f32[16,384]{1,0:T(8,128)S(1)} collective-permute-done((f32[16,384]{1,0:T(8,128)S(1)}, f32[16,384]{1,0:T(8,128)S(1)}, u32[]{:S(2)}, u32[]{:S(2)}) %collective-permute-start.8) | collective-permute-done | bytes 24608 | tf_op jit(solution)/shard_map/ppermute | solution.py:394
  147.1 10.1 %shard_map.47 = (f32[16,384]{1,0:T(8,128)S(1)}, f32[8,384]{1,0:T(8,128)S(1)}) custom-call(s32[1]{0:T(128)} %bitcast.slab_ref, f32[288,128]{1,0:T(8,128)S(1)} %collective-permute-done.6.refs_0_, f32[16,384]{1,0:T(8,128)S(1)} %collective-permute-done.8.refs_1_, f32[288,128]{1,0:T(8,128)S(1)} %get-tuple-element.59.refs_2_, ...), custom_call_target="tpu_custom_call" | custom-call | flops 4000000000 | bytes 1000000 | tf_op jit(solution)/shard_map/pallas_call | solution.py:381
  157.2 1.3 collective-permute-start.9
  158.5 1.5 collective-permute-done.9.got_ref
  160.0 0.5 shard_map.48
  160.5 1.3 collective-permute-start.10
  161.8 1.5 collective-permute-done.10.got_ref
  163.3 0.5 shard_map.49
  163.8 1.3 collective-permute-start.11
  165.1 1.5 collective-permute-done.11.got_ref
  166.6 0.5 shard_map.50
  167.1 1.3 collective-permute-start.12
  168.4 1.5 collective-permute-done.12.got_ref
  169.9 1.2 shard_map.51
  (3 shorter events, 0.0 us)
Async XLA Ops:
  0.0 45.4 %copy-start = (f32[2,192,384]{2,1,0:T(8,128)S(1)}, f32[2,192,384]{2,1,0:T(8,128)}, u32[]{:S(2)}) copy-start(f32[2,192,384]{2,1,0:T(8,128)} %coup_ref.3) | copy-start | bytes 1769476
  0.0 0.9 copy-start.1
  1.7 53.2 %all-to-all-start = ((f32[8,24,384]{2,1,0:T(8,128)}), f32[8,24,384]{2,1,0:T(8,128)S(1)}, u32[]{:S(2)}, u32[]{:S(2)}) async-start(f32[8,24,384]{2,1,0:T(8,128)} %shard_map.37), calls=%async_computation | async-start | bytes 589824 | tf_op jit(solution)/shard_map/all_to_all | solution.py:412
  45.4 23.6 %collective-permute-start.1 = (f32[192,384]{1,0:T(8,128)S(1)}, f32[192,384]{1,0:T(8,128)S(1)}, u32[]{:S(2)}, u32[]{:S(2)}) collective-permute-start(f32[192,384]{1,0:T(8,128)S(1)} %slice_bitcast_fusion), channel_id=1, source_target_pairs={{16,0},{32,16},{48,32},{64,48},{80,64},{96,80},{112,96},{128,112},... | collective-permute-start | bytes 884744 | tf_op jit(solution)/shard_map/ppermute | solution.py:432
  57.1 11.9 %copy-start.2 = (f32[2,8,384]{2,1,0:T(8,128)S(1)}, f32[2,8,384]{2,1,0:T(8,128)}, u32[]{:S(2)}) copy-start(f32[2,8,384]{2,1,0:T(8,128)} %src_ref.1) | copy-start | bytes 73732
  67.7 7.8 %collective-permute-start = (f32[288,128]{1,0:T(8,128)S(1)}, f32[288,128]{1,0:T(8,128)S(1)}, u32[]{:S(2)}, u32[]{:S(2)}) collective-permute-start(f32[288,128]{1,0:T(8,128)S(1)} %get-tuple-element.42.refs_1_), channel_id=1, source_target_pairs={{16,0},{48,32},{80,64},{112,96},{144,128},{176,160},{208,192},{240... | collective-permute-start | bytes 442376 | tf_op jit(solution)/shard_map/ppermute | solution.py:394
  73.3 14.7 %collective-permute-start.3 = (f32[912,128]{1,0:T(8,128)S(1)}, f32[912,128]{1,0:T(8,128)S(1)}, u32[]{:S(2)}, u32[]{:S(2)}) collective-permute-start(f32[912,128]{1,0:T(8,128)S(1)} %get-tuple-element.45.refs_2_), channel_id=1, source_target_pairs={{16,0},{48,32},{80,64},{112,96},{144,128},{176,160},{208,192},{240... | collective-permute-start | bytes 1400840 | tf_op jit(solution)/shard_map/ppermute | solution.py:394
  86.5 8.0 %collective-permute-start.2 = (f32[288,128]{1,0:T(8,128)S(1)}, f32[288,128]{1,0:T(8,128)S(1)}, u32[]{:S(2)}, u32[]{:S(2)}) collective-permute-start(f32[288,128]{1,0:T(8,128)S(1)} %get-tuple-element.46.refs_1_), channel_id=1, source_target_pairs={{32,0},{96,64},{160,128},{224,192},{33,1},{97,65},{161,129},{225,1... | collective-permute-start | bytes 442376 | tf_op jit(solution)/shard_map/ppermute | solution.py:394
  92.2 14.7 %collective-permute-start.5 = (f32[912,128]{1,0:T(8,128)S(1)}, f32[912,128]{1,0:T(8,128)S(1)}, u32[]{:S(2)}, u32[]{:S(2)}) collective-permute-start(f32[912,128]{1,0:T(8,128)S(1)} %get-tuple-element.49.refs_2_), channel_id=1, source_target_pairs={{32,0},{96,64},{160,128},{224,192},{33,1},{97,65},{161,129},{225,1... | collective-permute-start | bytes 1400840 | tf_op jit(solution)/shard_map/ppermute | solution.py:394
  105.5 11.0 %collective-permute-start.4 = (f32[288,128]{1,0:T(8,128)S(1)}, f32[288,128]{1,0:T(8,128)S(1)}, u32[]{:S(2)}, u32[]{:S(2)}) collective-permute-start(f32[288,128]{1,0:T(8,128)S(1)} %get-tuple-element.50.refs_1_), channel_id=1, source_target_pairs={{64,0},{192,128},{65,1},{193,129},{66,2},{194,130},{67,3},{195,131... | collective-permute-start | bytes 442376 | tf_op jit(solution)/shard_map/ppermute | solution.py:394
  111.2 17.7 %collective-permute-start.7 = (f32[912,128]{1,0:T(8,128)S(1)}, f32[912,128]{1,0:T(8,128)S(1)}, u32[]{:S(2)}, u32[]{:S(2)}) collective-permute-start(f32[912,128]{1,0:T(8,128)S(1)} %get-tuple-element.53.refs_2_), channel_id=1, source_target_pairs={{64,0},{192,128},{65,1},{193,129},{66,2},{194,130},{67,3},{195,131... | collective-permute-start | bytes 1400840 | tf_op jit(solution)/shard_map/ppermute | solution.py:394
  127.5 17.7 %collective-permute-start.6 = (f32[288,128]{1,0:T(8,128)S(1)}, f32[288,128]{1,0:T(8,128)S(1)}, u32[]{:S(2)}, u32[]{:S(2)}) collective-permute-start(f32[288,128]{1,0:T(8,128)S(1)} %get-tuple-element.54.refs_0_), channel_id=1, source_target_pairs={{128,0},{129,1},{130,2},{131,3},{132,4},{133,5},{134,6},{135,7},{1... | collective-permute-start | bytes 442376 | tf_op jit(solution)/shard_map/ppermute | solution.py:394
  132.6 14.5 %collective-permute-start.8 = (f32[16,384]{1,0:T(8,128)S(1)}, f32[16,384]{1,0:T(8,128)S(1)}, u32[]{:S(2)}, u32[]{:S(2)}) collective-permute-start(f32[16,384]{1,0:T(8,128)S(1)} %get-tuple-element.57.refs_2_), channel_id=1, source_target_pairs={{128,0},{129,1},{130,2},{131,3},{132,4},{133,5},{134,6},{135,7},{1... | collective-permute-start | bytes 73736 | tf_op jit(solution)/shard_map/ppermute | solution.py:394
  157.2 2.8 %collective-permute-start.9 = (f32[16,384]{1,0:T(8,128)S(1)}, f32[16,384]{1,0:T(8,128)S(1)}, u32[]{:S(2)}, u32[]{:S(2)}) collective-permute-start(f32[16,384]{1,0:T(8,128)S(1)} %get-tuple-element.63.prev_ref), channel_id=1, source_target_pairs={{0,128},{1,129},{2,130},{3,131},{4,132},{5,133},{6,134},{7,135},{8... | collective-permute-start | bytes 73736 | tf_op jit(solution)/shard_map/ppermute | solution.py:399
  160.5 2.8 %collective-permute-start.10 = (f32[16,384]{1,0:T(8,128)S(1)}, f32[16,384]{1,0:T(8,128)S(1)}, u32[]{:S(2)}, u32[]{:S(2)}) collective-permute-start(f32[16,384]{1,0:T(8,128)S(1)} %get-tuple-element.67.prev_ref), channel_id=1, source_target_pairs={{0,64},{128,192},{1,65},{129,193},{2,66},{130,194},{3,67},{131,195... | collective-permute-start | bytes 73736 | tf_op jit(solution)/shard_map/ppermute | solution.py:399
  163.8 2.8 %collective-permute-start.11 = (f32[16,384]{1,0:T(8,128)S(1)}, f32[16,384]{1,0:T(8,128)S(1)}, u32[]{:S(2)}, u32[]{:S(2)}) collective-permute-start(f32[16,384]{1,0:T(8,128)S(1)} %get-tuple-element.71.prev_ref), channel_id=1, source_target_pairs={{0,32},{64,96},{128,160},{192,224},{1,33},{65,97},{129,161},{193,2... | collective-permute-start | bytes 73736 | tf_op jit(solution)/shard_map/ppermute | solution.py:399
  167.1 2.8 %collective-permute-start.12 = (f32[16,384]{1,0:T(8,128)S(1)}, f32[16,384]{1,0:T(8,128)S(1)}, u32[]{:S(2)}, u32[]{:S(2)}) collective-permute-start(f32[16,384]{1,0:T(8,128)S(1)} %get-tuple-element.75.prev_ref), channel_id=1, source_target_pairs={{0,16},{32,48},{64,80},{96,112},{128,144},{160,176},{192,208},{224... | collective-permute-start | bytes 73736 | tf_op jit(solution)/shard_map/ppermute | solution.py:399
